TPU v7x, 32 devices: a whole 2x2x4 slice. The times are simulated.
32 devices in a mesh: seq: 8 (over y, x, core), ch: 4 (over z).
Axes of the slice: x: 2, y: 2, z: 4, core: 2. Of those that a mesh axis runs over, the one named last changes fastest.
Arguments:
- inputs: bfloat16 [256, 4096], P('ch', 'seq'), may hold values from -6 to 6
- w_value: bfloat16 [256, 256], P(None, 'ch'), may hold values from -0.375 to 0.375
- w_gate: bfloat16 [256, 256], P(None, 'ch'), may hold values from -0.375 to 0.375
- w_out: bfloat16 [256, 256], P('ch'), may hold values from -0.375 to 0.375
- filter_taps: float32 [256, 4096], P('ch', 'seq'), may hold values from -6 to 6
- grad_out: bfloat16 [256, 4096], P('ch', 'seq'), may hold values from -6 to 6
Outputs:
- d_inputs: bfloat16 [256, 4096], P('ch', 'seq')
- d_w_value: float32 [256, 256], P(None, 'ch')
- d_w_gate: float32 [256, 256], P(None, 'ch')
- d_w_out: float32 [256, 256], P('ch')
- d_filter: float32 [256, 4096], P('ch', 'seq')
All inputs are finite; a program needn't handle non-finite values.
Results may differ from a plain program's by a relative error of at most 0.015.
Values may be sent and summed in bfloat16 or wider, within the bound.
A program may use at most 64 MiB of HBM per device.

v0:
```python
import functools
import math

import jax
import jax.numpy as jnp
import numpy as np
from jax import lax
from jax.experimental import pallas as pl
from jax.experimental.pallas import tpu as pltpu
from jax.sharding import PartitionSpec as P

F32 = jnp.float32
BF16 = jnp.bfloat16
LANES = 128


def dft_tables(strides, lanes, chans):
    length = 2 * strides * lanes
    n1 = np.arange(strides)
    n2 = np.arange(lanes)
    half = np.arange(strides) + 0.5
    first = np.exp(-2j * np.pi * np.outer(half, n1) / (2 * strides))
    eye = np.eye(chans)
    first_re, first_im = np.kron(first.real, eye), np.kron(first.imag, eye)
    ahead = np.concatenate([first_re, first_im], 0)
    twist = np.repeat(np.exp(-2j * np.pi * np.outer(half, n2) / length), chans, axis=0)
    last = np.exp(-2j * np.pi * np.outer(n2, n2) / lanes)
    c, s = last.real, last.imag
    across = np.block([[c, s], [-s, c]])
    low = lambda a: jnp.asarray(a.astype(np.float32)).astype(BF16)
    wide = lambda a: jnp.asarray(a.astype(np.float32))
    return (
        low(ahead),
        low(ahead.T * (2.0 / length)),
        low(across),
        low(across.T),
        wide(np.stack([twist.real, twist.imag])),
    )


def each(count, step):
    if count <= 16:
        for k in range(count):
            step(k)
    else:
        lax.fori_loop(0, count, lambda k, carry: (step(k), carry)[1], 0)


def body(
    groups, rings,
    in_hbm, wv_hbm, wg_hbm, wo_hbm, filt_hbm, grad_hbm, ahead_hbm, back_hbm, across_hbm, return_hbm, twist_hbm,
    din_ref, dw_ref, dfil_ref,
    full_in, full_grad, got_filt, out_val, got_val, out_dif, got_dif,
    out_mix, got_mix, out_dv, got_dv, out_df, got_df,
    out_din, got_din, out_w, got_w, out_ws, got_ws, out_v, got_v, out_vs, got_vs,
    wv_ref, wg_ref, wo_ref, filt_ref, ahead_ref, back_ref, across_ref, return_ref, twist_ref,
    seq_send, seq_recv, ch_send, ch_recv, line_send, line_recv, table_sem, fetch_sem,
):
    me = lax.axis_index("seq")
    mc = lax.axis_index("ch")
    ch_rows, tokens = in_hbm.shape
    chans = ch_rows // groups
    tiles = tokens // LANES
    width = full_in.shape[0] * ch_rows
    barrier = pltpu.get_barrier_semaphore()

    def seq_peer(k):
        return lax.rem(me + k, groups)

    def ch_peer(k):
        return lax.rem(mc + k, rings)

    each(groups - 1, lambda k: pl.semaphore_signal(
        barrier, inc=1, device_id={"seq": seq_peer(k + 1)}, device_id_type=pl.DeviceIdType.MESH))
    each(rings - 1, lambda k: pl.semaphore_signal(
        barrier, inc=1, device_id={"ch": ch_peer(k + 1)}, device_id_type=pl.DeviceIdType.MESH))
    tables = [
        pltpu.make_async_copy(src, dst, table_sem.at[i])
        for i, (src, dst) in enumerate((
            (ahead_hbm, ahead_ref), (twist_hbm, twist_ref), (across_hbm, across_ref),
            (return_hbm, return_ref), (back_hbm, back_ref),
            (wv_hbm, wv_ref), (wg_hbm, wg_ref), (wo_hbm, wo_ref)))
    ]
    fetches = [
        pltpu.make_async_copy(src, dst, fetch_sem.at[i])
        for i, (src, dst) in enumerate((
            (in_hbm, full_in.at[mc]), (grad_hbm, full_grad.at[mc]), (filt_hbm, filt_ref)))
    ]
    for copy in fetches + tables:
        copy.start()
    pl.semaphore_wait(barrier, groups + rings - 2)

    def seq_copy(stage, src, dst, k, pick):
        return pltpu.make_async_remote_copy(
            src_ref=src.at[seq_peer(k)] if pick else src,
            dst_ref=dst.at[me],
            send_sem=seq_send.at[stage, k],
            recv_sem=seq_recv.at[stage, k],
            device_id={"seq": seq_peer(k)},
            device_id_type=pl.DeviceIdType.MESH,
        )

    def ch_copy(src, dst, k):
        return pltpu.make_async_remote_copy(
            src_ref=src.at[ch_peer(k)],
            dst_ref=dst.at[mc],
            send_sem=ch_send.at[k],
            recv_sem=ch_recv.at[k],
            device_id={"ch": ch_peer(k)},
            device_id_type=pl.DeviceIdType.MESH,
        )

    def seq_start(stage, src, dst, pick=True):
        each(groups - 1, lambda k: seq_copy(stage, src, dst, k + 1, pick).start())

    def seq_wait(stage, src, dst, pick=True):
        each(groups - 1, lambda k: seq_copy(stage, src, dst, k + 1, pick).wait_recv())

    def seq_done(stage, src, dst, pick=True):
        each(groups - 1, lambda k: seq_copy(stage, src, dst, k + 1, pick).wait_send())

    wholes = (full_in, full_grad)

    def hop(array, block, step):
        return pltpu.make_async_remote_copy(
            src_ref=wholes[array].at[block],
            dst_ref=wholes[array].at[block],
            send_sem=line_send.at[array, (step + 1) // 2, block],
            recv_sem=line_recv.at[array, block],
            device_id={"ch": mc + step},
            device_id_type=pl.DeviceIdType.MESH,
        )

    def can(step):
        return mc < rings - 1 if step == 1 else mc > 0

    def present(step, far):
        return mc >= far if step == 1 else mc < rings - far

    def line_open(array):
        for step in (1, -1):
            @pl.when(can(step))
            def _():
                hop(array, mc, step).start()

    def line_take(array, far):
        for step in (1, -1):
            @pl.when(present(step, far))
            def _():
                hop(array, mc - step * far, step).wait_recv()
                if far < rings - 1:
                    @pl.when(can(step))
                    def _():
                        hop(array, mc - step * far, step).start()

    def line_close(array):
        for step in (1, -1):
            @pl.when(can(step))
            def _():
                hop(array, mc, step).wait_send()
                for far in range(1, rings - 1):
                    @pl.when(present(step, far))
                    def _():
                        hop(array, mc - step * far, step).wait_send()

    fetches[0].wait()
    line_open(0)
    fetches[1].wait()
    line_open(1)
    fetches[2].wait()
    seq_start(0, filt_ref, got_filt)
    got_filt[me] = filt_ref[me]

    def by_owner(x):
        x = x.reshape(groups, chans, tokens)
        return jnp.concatenate([x[:, :, j * LANES:(j + 1) * LANES] for j in range(tiles)], axis=1)

    def by_token(x):
        x = x.astype(F32)
        x = jnp.concatenate([x[:, j * chans:(j + 1) * chans, :] for j in range(tiles)], axis=2)
        return x.reshape(ch_rows, tokens)

    def stacked(ref):
        return jnp.concatenate([ref[p] for p in range(groups)], axis=0).astype(BF16)

    rows = ahead_ref.shape[1]

    def dot(a, b):
        return jnp.dot(a, b, preferred_element_type=F32)

    def spectrum(x):
        first = dot(ahead_ref[...], x)
        re, im = first[:rows], first[rows:]
        tw_re, tw_im = twist_ref[0], twist_ref[1]
        mid = jnp.concatenate([re * tw_re - im * tw_im, re * tw_im + im * tw_re], axis=1).astype(BF16)
        out = dot(mid, across_ref[...])
        return out[:, :LANES], out[:, LANES:]

    def signal(re, im):
        mid = dot(jnp.concatenate([re, im], axis=1).astype(BF16), return_ref[...])
        re, im = mid[:, :LANES], mid[:, LANES:]
        tw_re, tw_im = twist_ref[0], twist_ref[1]
        tall = jnp.concatenate([re * tw_re + im * tw_im, im * tw_re - re * tw_im], axis=0).astype(BF16)
        return dot(back_ref[...], tall).reshape(groups, tiles * chans, LANES)

    over_first = (((0,), (0,)), ((), ()))
    over_last = (((1,), (1,)), ((), ()))
    for far in range(1, rings - 1):
        line_take(0, far)
        line_take(1, far)

    for table in tables:
        table.wait()
    seq_wait(0, filt_ref, got_filt)
    by_tile = jnp.concatenate(
        [got_filt[p][:, j * LANES:(j + 1) * LANES] for p in range(groups) for j in range(tiles)], axis=0)
    f_re, f_im = spectrum(by_tile.astype(BF16))

    line_take(0, rings - 1)
    x_in = full_in[...].reshape(width, tokens)
    value = dot(wv_ref[...], x_in)
    out_val[...] = by_owner(value).astype(BF16)
    seq_start(1, out_val, got_val)
    got_val[me] = out_val[me]
    gate = dot(wg_ref[...], x_in)

    line_take(1, rings - 1)
    x_grad = full_grad[...].reshape(width, tokens)
    d_gated = dot(wo_ref[...], x_grad)
    out_dif[...] = by_owner(d_gated * gate).astype(BF16)
    seq_start(2, out_dif, got_dif)
    got_dif[me] = out_dif[me]

    seq_wait(1, out_val, got_val)
    v_re, v_im = spectrum(stacked(got_val))
    out_mix[...] = signal(f_re * v_re - f_im * v_im, f_re * v_im + f_im * v_re).astype(BF16)
    seq_start(3, out_mix, got_mix)
    got_mix[me] = out_mix[me]

    seq_wait(2, out_dif, got_dif)
    g_re, g_im = spectrum(stacked(got_dif))
    out_dv[...] = signal(f_re * g_re + f_im * g_im, f_re * g_im - f_im * g_re).astype(BF16)
    seq_start(4, out_dv, got_dv)
    got_dv[me] = out_dv[me]
    out_df[...] = signal(v_re * g_re + v_im * g_im, v_re * g_im - v_im * g_re).astype(BF16)
    seq_start(5, out_df, got_df)
    got_df[me] = out_df[me]

    parts = width // LANES

    def by_share(x):
        x = x.reshape(groups, chans, width)
        return jnp.concatenate([x[:, :, j * LANES:(j + 1) * LANES] for j in range(parts)], axis=1)

    def by_width(x):
        return jnp.concatenate([x[:, j * chans:(j + 1) * chans, :] for j in range(parts)], axis=2).reshape(ch_rows, width)

    def total(ref):
        out = ref[0].astype(F32)
        for p in range(1, ref.shape[0]):
            out = out + ref[p].astype(F32)
        return out.astype(BF16)

    seq_wait(3, out_mix, got_mix)
    mixed = by_token(got_mix[...])
    gated_out = (gate * mixed).astype(BF16)
    d_gate = (d_gated * mixed).astype(BF16)
    gate_term = lax.dot_general(d_gate, x_in, over_last, preferred_element_type=F32)
    out_term = lax.dot_general(gated_out, x_grad, over_last, preferred_element_type=F32)
    out_w[...] = jnp.concatenate([by_share(gate_term), by_share(out_term)], axis=1).astype(BF16)
    seq_start(6, out_w, got_w)
    got_w[me] = out_w[me]
    from_gate = lax.dot_general(wg_ref[...], d_gate, over_first, preferred_element_type=F32)

    seq_wait(4, out_dv, got_dv)
    d_value = by_token(got_dv[...]).astype(BF16)
    value_term = lax.dot_general(d_value, x_in, over_last, preferred_element_type=F32)
    out_v[...] = by_share(value_term).astype(BF16)
    seq_start(8, out_v, got_v)
    d_in = lax.dot_general(wv_ref[...], d_value, over_first, preferred_element_type=F32) + from_gate
    out_din[...] = d_in.reshape(rings, ch_rows, tokens).astype(BF16)
    each(rings - 1, lambda k: ch_copy(out_din, got_din, k + 1).start())
    got_v[me] = out_v[me]
    got_din[mc] = out_din[mc]

    seq_wait(6, out_w, got_w)
    out_ws[...] = total(got_w)
    seq_start(7, out_ws, got_ws, False)
    got_ws[me] = out_ws[...]

    seq_wait(5, out_df, got_df)
    dfil_ref[...] = by_token(got_df[...]).astype(BF16)

    seq_wait(8, out_v, got_v)
    out_vs[...] = total(got_v)
    seq_start(9, out_vs, got_vs, False)
    got_vs[me] = out_vs[...]

    seq_wait(7, out_ws, got_ws, False)
    half = parts * chans
    summed = got_ws[...].astype(F32)
    dw_ref[1] = by_width(summed[:, :half, :]).astype(BF16)
    dw_ref[2] = by_width(summed[:, half:, :]).astype(BF16)
    each(rings - 1, lambda k: ch_copy(out_din, got_din, k + 1).wait_recv())
    din_ref[...] = total(got_din)
    seq_wait(9, out_vs, got_vs, False)
    dw_ref[0] = by_width(got_vs[...].astype(F32)).astype(BF16)

    line_close(0)
    line_close(1)
    each(rings - 1, lambda k: ch_copy(out_din, got_din, k + 1).wait_send())
    for stage, src, dst, pick in (
        (0, filt_ref, got_filt, True), (1, out_val, got_val, True), (2, out_dif, got_dif, True),
        (3, out_mix, got_mix, True), (4, out_dv, got_dv, True), (5, out_df, got_df, True),
        (6, out_w, got_w, True), (7, out_ws, got_ws, False), (8, out_v, got_v, True), (9, out_vs, got_vs, False),
    ):
        seq_done(stage, src, dst, pick)


def finish(scale, din_ref, dw_ref, dfil_ref, din_out, dwv_out, dwg_out, dwo_out, dfil_out):
    din_out[...] = din_ref[...]
    dwv_out[...] = dw_ref[0].astype(F32) * scale
    dwg_out[...] = dw_ref[1].astype(F32) * scale
    dwo_out[...] = dw_ref[2].astype(F32) * scale
    dfil_out[...] = dfil_ref[...].astype(F32) * scale


def solution(mesh):
    groups, rings = mesh.shape["seq"], mesh.shape["ch"]

    def on_device(inputs, w_value, w_gate, w_out, filter_taps, grad_out):
        ch_rows, tokens = inputs.shape
        width = w_value.shape[0]
        chans, tiles, parts = ch_rows // groups, tokens // LANES, width // LANES
        tables = dft_tables(groups * tiles, LANES, chans)
        scale = 1.0 / math.sqrt(tokens * groups)
        vmem = pl.BlockSpec(memory_space=pltpu.VMEM)
        hbm = pl.BlockSpec(memory_space=pltpu.HBM)
        block = pltpu.VMEM((groups, tiles * chans, LANES), BF16)
        whole = pltpu.VMEM((rings, ch_rows, tokens), BF16)
        share = lambda count: [
            pltpu.VMEM((groups, count * parts * chans, LANES), BF16),
            pltpu.VMEM((groups, count * parts * chans, LANES), BF16),
            pltpu.VMEM((count * parts * chans, LANES), BF16),
            pltpu.VMEM((groups, count * parts * chans, LANES), BF16),
        ]
        tokens_out = jax.ShapeDtypeStruct((ch_rows, tokens), F32)
        weight_out = jax.ShapeDtypeStruct((ch_rows, width), F32)
        d_inputs, d_weights, d_filter = pl.pallas_call(
            functools.partial(body, groups, rings),
            out_shape=(
                jax.ShapeDtypeStruct((ch_rows, tokens), BF16),
                jax.ShapeDtypeStruct((3, ch_rows, width), BF16),
                jax.ShapeDtypeStruct((ch_rows, tokens), BF16),
            ),
            in_specs=[hbm] * 11,
            out_specs=(vmem,) * 3,
            scratch_shapes=[whole, whole, pltpu.VMEM((groups, chans, tokens), F32)] + [block] * 10
            + [whole, whole] + share(2) + share(1)
            + [pltpu.VMEM((ch_rows, width), BF16)] * 3 + [pltpu.VMEM((groups, chans, tokens), F32)]
            + [pltpu.VMEM(table.shape, table.dtype) for table in tables] + [
                pltpu.SemaphoreType.DMA((10, groups)),
                pltpu.SemaphoreType.DMA((10, groups)),
                pltpu.SemaphoreType.DMA((rings,)),
                pltpu.SemaphoreType.DMA((rings,)),
                pltpu.SemaphoreType.DMA((2, 2, rings)),
                pltpu.SemaphoreType.DMA((2, rings)),
                pltpu.SemaphoreType.DMA((8,)),
                pltpu.SemaphoreType.DMA((3,)),
            ],
            compiler_params=pltpu.CompilerParams(collective_id=0, has_side_effects=True),
        )(
            inputs, w_value.T, w_gate.T, w_out, filter_taps.reshape(groups, chans, tokens), grad_out, *tables,
        )
        d_inputs, d_w_value, d_w_gate, d_w_out, d_filter = pl.pallas_call(
            functools.partial(finish, scale),
            out_shape=(
                jax.ShapeDtypeStruct((ch_rows, tokens), BF16), weight_out, weight_out, weight_out, tokens_out,
            ),
            in_specs=[vmem] * 3,
            out_specs=(vmem,) * 5,
        )(d_inputs, d_weights, d_filter)
        return d_inputs, d_w_value.T, d_w_gate.T, d_w_out, d_filter

    return jax.shard_map(
        on_device,
        mesh=mesh,
        in_specs=(P("ch", "seq"), P(None, "ch"), P(None, "ch"), P("ch", None), P("ch", "seq"), P("ch", "seq")),
        out_specs=(P("ch", "seq"), P(None, "ch"), P(None, "ch"), P("ch", None), P("ch", "seq")),
        check_vma=False,
    )
```

profile of v0, /device:TPU:0, one launch (start us, length us, event | category | flops | bytes accessed | tf_op | source)
XLA Modules:
  0.0 36.1 jit_solution(7987994352595974454)
XLA Ops:
  0.6 33.7 %shard_map.146 = (bf16[64,512]{1,0:T(8,128)(2,1)}, bf16[3,64,256]{2,1,0:T(8,128)(2,1)}, bf16[64,512]{1,0:T(8,128)(2,1)}) custom-call(bf16[64,512]{1,0:T(8,128)(2,1)} %in_hbm.1, bf16[64,256]{1,0:T(8,128)(2,1)} %bitcast.6, bf16[64,256]{1,0:T(8,128)(2,1)} %bitcast.7, bf16[64,256]{1,0:T(8,128)(2,1)} %wo_hbm.1, f32[8,8,512]{2,1,0:T(8,128)} %bitcast.5, ...), custom_call_target="tpu_custom_call" | custom-call | tf_op jit(solution)/shard_map/pallas_call | solution.py:349
  34.4 1.7 %shard_map.147 = (bf16[64,512]{1,0:T(8,128)(2,1)}, f32[64,256]{1,0:T(8,128)}, f32[64,256]{1,0:T(8,128)}, f32[64,256]{1,0:T(8,128)}, f32[64,512]{1,0:T(8,128)}) custom-call(bf16[64,512]{1,0:T(8,128)(2,1)} %get-tuple-element.13.din_ref, bf16[3,64,256]{2,1,0:T(8,128)(2,1)} %get-tuple-element.14.dw_ref, bf16[64,512]{1,0:T(8,128)(2,1)} %get-tuple-element.15.dfil_ref), custom_call_target="tpu_custom_call" | custom-call | tf_op jit(solution)/shard_map/pallas_call | solution.py:375
where the time goes:
time: 36.2 us; the launch traced here: 36.1 us
  Pallas kernels  35.4 us (98%)
  between operations  0.64 us (2%)
    pallas_call x1, Pallas kernels, on_device(): pl.pallas_call(functools.partial(body, groups, rings), out_shape=(jax.Sha...  33.7 us
    pallas_call x1, Pallas kernels, on_device(): pl.pallas_call(functools.partial(finish, scale), out_shape=(jax.ShapeDtyp...  1.67 us

commit v1 on v0

--- a/solution.py
+++ b/solution.py
@@ -46,6 +46,12 @@
         lax.fori_loop(0, count, lambda k, carry: (step(k), carry)[1], 0)
 
 
+def near(count):
+    if count & (count - 1):
+        return None
+    return [1 << b for b in range(count.bit_length() - 1)]
+
+
 def body(
     groups, rings,
     in_hbm, wv_hbm, wg_hbm, wo_hbm, filt_hbm, grad_hbm, ahead_hbm, back_hbm, across_hbm, return_hbm, twist_hbm,
@@ -54,7 +60,7 @@
     out_mix, got_mix, out_dv, got_dv, out_df, got_df,
     out_din, got_din, out_w, got_w, out_ws, got_ws, out_v, got_v, out_vs, got_vs,
     wv_ref, wg_ref, wo_ref, filt_ref, ahead_ref, back_ref, across_ref, return_ref, twist_ref,
-    seq_send, seq_recv, ch_send, ch_recv, line_send, line_recv, table_sem, fetch_sem,
+    seq_send, seq_recv, ch_send, ch_recv, line_send, line_recv, table_sem, fetch_sem, round_sem,
 ):
     me = lax.axis_index("seq")
     mc = lax.axis_index("ch")
@@ -70,10 +76,22 @@
     def ch_peer(k):
         return lax.rem(mc + k, rings)
 
-    each(groups - 1, lambda k: pl.semaphore_signal(
-        barrier, inc=1, device_id={"seq": seq_peer(k + 1)}, device_id_type=pl.DeviceIdType.MESH))
-    each(rings - 1, lambda k: pl.semaphore_signal(
-        barrier, inc=1, device_id={"ch": ch_peer(k + 1)}, device_id_type=pl.DeviceIdType.MESH))
+    hops = near(groups)
+
+    def can(step):
+        return mc < rings - 1 if step == 1 else mc > 0
+
+    def greet(semaphore):
+        for hop_by in hops:
+            pl.semaphore_signal(
+                semaphore, inc=1, device_id={"seq": me ^ hop_by}, device_id_type=pl.DeviceIdType.MESH)
+
+    greet(barrier)
+    for step in (1, -1):
+        @pl.when(can(step))
+        def _():
+            pl.semaphore_signal(
+                barrier, inc=1, device_id={"ch": mc + step}, device_id_type=pl.DeviceIdType.MESH)
     tables = [
         pltpu.make_async_copy(src, dst, table_sem.at[i])
         for i, (src, dst) in enumerate((
@@ -88,14 +106,23 @@
     ]
     for copy in fetches + tables:
         copy.start()
-    pl.semaphore_wait(barrier, groups + rings - 2)
+    between = (mc > 0) & (mc < rings - 1)
+
+    @pl.when(between)
+    def _():
+        pl.semaphore_wait(barrier, len(hops) + 2)
+
+    @pl.when(jnp.logical_not(between))
+    def _():
+        pl.semaphore_wait(barrier, len(hops) + 1)
+
 
     def seq_copy(stage, src, dst, k, pick):
         return pltpu.make_async_remote_copy(
             src_ref=src.at[seq_peer(k)] if pick else src,
             dst_ref=dst.at[me],
-            send_sem=seq_send.at[stage, k],
-            recv_sem=seq_recv.at[stage, k],
+            send_sem=seq_send.at[stage],
+            recv_sem=seq_recv.at[stage],
             device_id={"seq": seq_peer(k)},
             device_id_type=pl.DeviceIdType.MESH,
         )
@@ -104,8 +131,8 @@
         return pltpu.make_async_remote_copy(
             src_ref=src.at[ch_peer(k)],
             dst_ref=dst.at[mc],
-            send_sem=ch_send.at[k],
-            recv_sem=ch_recv.at[k],
+            send_sem=ch_send.at[0],
+            recv_sem=ch_recv.at[0],
             device_id={"ch": ch_peer(k)},
             device_id_type=pl.DeviceIdType.MESH,
         )
@@ -113,11 +140,15 @@
     def seq_start(stage, src, dst, pick=True):
         each(groups - 1, lambda k: seq_copy(stage, src, dst, k + 1, pick).start())
 
+    def took(ref, count, semaphore):
+        blocks = ref.at[pl.ds(0, count)]
+        pltpu.make_async_copy(blocks, blocks, semaphore).wait()
+
     def seq_wait(stage, src, dst, pick=True):
-        each(groups - 1, lambda k: seq_copy(stage, src, dst, k + 1, pick).wait_recv())
+        took(dst, groups - 1, seq_recv.at[stage])
 
     def seq_done(stage, src, dst, pick=True):
-        each(groups - 1, lambda k: seq_copy(stage, src, dst, k + 1, pick).wait_send())
+        took(dst, groups - 1, seq_send.at[stage])
 
     wholes = (full_in, full_grad)
 
@@ -131,9 +162,6 @@
             device_id_type=pl.DeviceIdType.MESH,
         )
 
-    def can(step):
-        return mc < rings - 1 if step == 1 else mc > 0
-
     def present(step, far):
         return mc >= far if step == 1 else mc < rings - far
 
@@ -167,6 +195,9 @@
     line_open(0)
     fetches[1].wait()
     line_open(1)
+    for turn in range(len(hops) - 1):
+        greet(round_sem.at[turn])
+        pl.semaphore_wait(round_sem.at[turn], len(hops))
     fetches[2].wait()
     seq_start(0, filt_ref, got_filt)
     got_filt[me] = filt_ref[me]
@@ -301,14 +332,14 @@
     summed = got_ws[...].astype(F32)
     dw_ref[1] = by_width(summed[:, :half, :]).astype(BF16)
     dw_ref[2] = by_width(summed[:, half:, :]).astype(BF16)
-    each(rings - 1, lambda k: ch_copy(out_din, got_din, k + 1).wait_recv())
+    took(got_din, rings - 1, ch_recv.at[0])
     din_ref[...] = total(got_din)
     seq_wait(9, out_vs, got_vs, False)
     dw_ref[0] = by_width(got_vs[...].astype(F32)).astype(BF16)
 
     line_close(0)
     line_close(1)
-    each(rings - 1, lambda k: ch_copy(out_din, got_din, k + 1).wait_send())
+    took(got_din, rings - 1, ch_send.at[0])
     for stage, src, dst, pick in (
         (0, filt_ref, got_filt, True), (1, out_val, got_val, True), (2, out_dif, got_dif, True),
         (3, out_mix, got_mix, True), (4, out_dv, got_dv, True), (5, out_df, got_df, True),
@@ -349,9 +380,9 @@
         d_inputs, d_weights, d_filter = pl.pallas_call(
             functools.partial(body, groups, rings),
             out_shape=(
-                jax.ShapeDtypeStruct((ch_rows, tokens), BF16),
-                jax.ShapeDtypeStruct((3, ch_rows, width), BF16),
-                jax.ShapeDtypeStruct((ch_rows, tokens), BF16),
+                pltpu.VMEM((ch_rows, tokens), BF16),
+                pltpu.VMEM((3, ch_rows, width), BF16),
+                pltpu.VMEM((ch_rows, tokens), BF16),
             ),
             in_specs=[hbm] * 11,
             out_specs=(vmem,) * 3,
@@ -359,14 +390,15 @@
             + [whole, whole] + share(2) + share(1)
             + [pltpu.VMEM((ch_rows, width), BF16)] * 3 + [pltpu.VMEM((groups, chans, tokens), F32)]
             + [pltpu.VMEM(table.shape, table.dtype) for table in tables] + [
-                pltpu.SemaphoreType.DMA((10, groups)),
-                pltpu.SemaphoreType.DMA((10, groups)),
-                pltpu.SemaphoreType.DMA((rings,)),
-                pltpu.SemaphoreType.DMA((rings,)),
+                pltpu.SemaphoreType.DMA((10,)),
+                pltpu.SemaphoreType.DMA((10,)),
+                pltpu.SemaphoreType.DMA((1,)),
+                pltpu.SemaphoreType.DMA((1,)),
                 pltpu.SemaphoreType.DMA((2, 2, rings)),
                 pltpu.SemaphoreType.DMA((2, rings)),
                 pltpu.SemaphoreType.DMA((8,)),
                 pltpu.SemaphoreType.DMA((3,)),
+                pltpu.SemaphoreType.REGULAR((max(len(near(groups)) - 1, 1),)),
             ],
             compiler_params=pltpu.CompilerParams(collective_id=0, has_side_effects=True),
         )(
@@ -379,6 +411,7 @@
             ),
             in_specs=[vmem] * 3,
             out_specs=(vmem,) * 5,
+            compiler_params=pltpu.CompilerParams(vmem_limit_bytes=8 << 20),
         )(d_inputs, d_weights, d_filter)
         return d_inputs, d_w_value.T, d_w_gate.T, d_w_out, d_filter
 

time: 36.2 us -> 31.8 us (0.88)
  Pallas kernels: 35.4 us -> 31 us
    pallas_call x1, Pallas kernels: 33.7 us -> 30.3 us  [on_device(): pl.pallas_call(functools.partial(body, groups, rings), out_shape=(pltpu.V...]
    pallas_call x1, Pallas kernels: 1.67 us -> 0.76 us  [on_device(): pl.pallas_call(functools.partial(finish, scale), out_shape=(jax.ShapeDtyp...]
where the time goes in v1:
time: 31.8 us; the launch traced here: 31.7 us
  Pallas kernels  31 us (97%)
  between operations  0.64 us (2%)
    pallas_call x1, Pallas kernels, on_device(): pl.pallas_call(functools.partial(body, groups, rings), out_shape=(pltpu.V...  30.3 us
    pallas_call x1, Pallas kernels, on_device(): pl.pallas_call(functools.partial(finish, scale), out_shape=(jax.ShapeDtyp...  0.76 us

profile of v1, /device:TPU:0, one launch (start us, length us, event | category | flops | bytes accessed | tf_op | source)
XLA Modules:
  0.0 31.7 jit_solution(10573555931157904677)
XLA Ops:
  0.6 30.3 %shard_map.146 = (bf16[64,512]{1,0:T(8,128)(2,1)S(1)}, bf16[3,64,256]{2,1,0:T(8,128)(2,1)S(1)}, bf16[64,512]{1,0:T(8,128)(2,1)S(1)}) custom-call(bf16[64,512]{1,0:T(8,128)(2,1)} %in_hbm.1, bf16[64,256]{1,0:T(8,128)(2,1)} %bitcast.6, bf16[64,256]{1,0:T(8,128)(2,1)} %bitcast.7, bf16[64,256]{1,0:T(8,128)(2,1)} %wo_hbm.1, f32[8,8,512]{2,1,0:T(8,128)} %bitcast.5, ...), custom_call_target="tpu_custom_call" | custom-call | tf_op jit(solution)/shard_map/pallas_call | solution.py:380
  30.9 0.8 %shard_map.147 = (bf16[64,512]{1,0:T(8,128)(2,1)}, f32[64,256]{1,0:T(8,128)}, f32[64,256]{1,0:T(8,128)}, f32[64,256]{1,0:T(8,128)}, f32[64,512]{1,0:T(8,128)}) custom-call(bf16[64,512]{1,0:T(8,128)(2,1)S(1)} %get-tuple-element.13.din_ref, bf16[3,64,256]{2,1,0:T(8,128)(2,1)S(1)} %get-tuple-element.14.dw_ref, bf16[64,512]{1,0:T(8,128)(2,1)S(1)} %get-tuple-element.15.dfil_ref), custom_call_target="tpu_custom_call" | custom-call | tf_op jit(solution)/shard_map/pallas_call | solution.py:407

commit v2 on v1

v2 whole, which is shorter than its diff:
```python
import functools
import math

import jax
import jax.numpy as jnp
import numpy as np
from jax import lax
from jax.experimental import pallas as pl
from jax.experimental.pallas import tpu as pltpu
from jax.sharding import PartitionSpec as P

F32 = jnp.float32
BF16 = jnp.bfloat16
LANES = 128


def dft_tables(strides, lanes, chans):
    length = 2 * strides * lanes
    n1 = np.arange(strides)
    n2 = np.arange(lanes)
    half = np.arange(strides) + 0.5
    first = np.exp(-2j * np.pi * np.outer(half, n1) / (2 * strides))
    eye = np.eye(chans)
    first_re, first_im = np.kron(first.real, eye), np.kron(first.imag, eye)
    ahead = np.concatenate([first_re, first_im], 0)
    twist = np.repeat(np.exp(-2j * np.pi * np.outer(half, n2) / length), chans, axis=0)
    last = np.exp(-2j * np.pi * np.outer(n2, n2) / lanes)
    c, s = last.real, last.imag
    across = np.block([[c, s], [-s, c]])
    low = lambda a: jnp.asarray(a.astype(np.float32)).astype(BF16)
    wide = lambda a: jnp.asarray(a.astype(np.float32))
    return (
        low(ahead),
        low(ahead.T * (2.0 / length)),
        low(across),
        low(across.T),
        wide(np.stack([twist.real, twist.imag])),
    )


def each(count, step):
    if count <= 16:
        for k in range(count):
            step(k)
    else:
        lax.fori_loop(0, count, lambda k, carry: (step(k), carry)[1], 0)


def near(count):
    return [1 << b for b in range(count.bit_length() - 1)]


def body(
    groups, rings,
    in_hbm, wv_hbm, wg_hbm, wo_hbm, filt_hbm, grad_hbm, ahead_hbm, back_hbm, across_hbm, return_hbm, twist_hbm,
    din_ref, dw_ref, dfil_ref,
    full_in, full_grad, filt_ref, weights, out_filt, got_filt, out_val, got_val, out_dif, got_dif,
    out_mix, got_mix, out_dv, got_dv, out_df, got_df,
    out_din, got_din, out_w, got_w, out_ws, got_ws, out_v, got_v, out_vs, got_vs,
    ahead_ref, back_ref, across_ref, return_ref, twist_ref,
    seq_send, seq_recv, din_send, din_recv, line_send, line_recv, weight_send, weight_recv,
    table_sem, fetch_sem, round_sem,
):
    me = lax.axis_index("seq")
    mc = lax.axis_index("ch")
    ch_rows, tokens = in_hbm.shape
    chans = ch_rows // groups
    tiles = tokens // LANES
    width = full_in.shape[0] * ch_rows
    parts = width // LANES
    half = rings // 2
    right = lax.div(mc, half)
    toward = 1 - 2 * right
    worker = half - 1 + right
    other = half - right
    slot = (worker - mc) * toward
    works = slot == 0
    rests = slot > 0
    between = (mc > 0) & (mc < rings - 1)
    barrier = pltpu.get_barrier_semaphore()
    hops = near(groups)

    def can(step):
        return mc < rings - 1 if step == 1 else mc > 0

    def greet(semaphore):
        for step in (1, -1):
            @pl.when(can(step))
            def _():
                pl.semaphore_signal(
                    semaphore, inc=1, device_id={"ch": mc + step}, device_id_type=pl.DeviceIdType.MESH)
        for hop_by in hops:
            pl.semaphore_signal(
                semaphore, inc=1, device_id={"seq": me ^ hop_by}, device_id_type=pl.DeviceIdType.MESH)

    def greeted(semaphore):
        @pl.when(between)
        def _():
            pl.semaphore_wait(semaphore, len(hops) + 2)

        @pl.when(jnp.logical_not(between))
        def _():
            pl.semaphore_wait(semaphore, len(hops) + 1)

    greet(barrier)
    fetches = [
        pltpu.make_async_copy(src, dst, fetch_sem.at[i])
        for i, (src, dst) in enumerate((
            (in_hbm, full_in.at[mc]), (grad_hbm, full_grad.at[mc]),
            (wv_hbm, weights.at[0, 0]), (wg_hbm, weights.at[0, 1]), (wo_hbm, weights.at[0, 2]),
            (filt_hbm, filt_ref)))
    ]
    tables = [
        pltpu.make_async_copy(src, dst, table_sem.at[i])
        for i, (src, dst) in enumerate((
            (ahead_hbm, ahead_ref), (twist_hbm, twist_ref), (across_hbm, across_ref),
            (return_hbm, return_ref), (back_hbm, back_ref)))
    ]
    for copy in fetches:
        copy.start()

    @pl.when(works)
    def _():
        for copy in tables:
            copy.start()

    greeted(barrier)

    def send(src, dst, sems, seq, ch):
        return pltpu.make_async_remote_copy(
            src_ref=src, dst_ref=dst, send_sem=sems[0], recv_sem=sems[1],
            device_id={"seq": seq, "ch": ch}, device_id_type=pl.DeviceIdType.MESH)

    def stage_sems(stage):
        return seq_send.at[stage], seq_recv.at[stage]

    def seq_peer(k):
        return lax.rem(me + k, groups)

    def took(ref, count, semaphore):
        blocks = ref.at[pl.ds(0, count)]
        pltpu.make_async_copy(blocks, blocks, semaphore).wait()

    def scatter(stage, src, dst, ch, skip, base=0):
        each(groups - skip, lambda k: send(
            src.at[base + seq_peer(k + skip)], dst, stage_sems(stage), seq_peer(k + skip), ch).start())

    def spread(stage, src, dst):
        each(groups - 1, lambda k: send(
            src, dst.at[me], stage_sems(stage), seq_peer(k + 1), mc).start())

    def to_planes(stage, src, dst):
        for s in range(half):
            scatter(stage, src, dst.at[me], mc - toward * s, 1 if s == 0 else 0, s * groups)
        dst[me] = src[me]

    wholes = (full_in, full_grad)

    def hop(array, block, k):
        return send(
            wholes[array].at[block], wholes[array].at[block],
            (line_send.at[array, k], line_recv.at[array, block]), me, mc + toward)

    def pass_on(array):
        for k in range(1, half):
            @pl.when(slot < half - k)
            def _():
                hop(array, mc - toward * k, k).wait_recv()
                hop(array, mc - toward * k, k).start()

    def take_inner(array):
        for k in range(half):
            hop(array, other + toward * k, 0).wait_recv()

    def weight_copy(kind, s):
        return send(weights.at[0, kind], weights.at[s, kind], (weight_send.at[kind], weight_recv.at[s, kind]), me, worker)

    for array in range(2):
        fetches[array].wait()
        hop(array, mc, 0).start()
    for kind in range(3):
        fetches[2 + kind].wait()

        @pl.when(rests)
        def _():
            weight_copy(kind, slot).start()

    for turn in range(len(hops) + half - 2):
        greet(round_sem.at[turn])
        greeted(round_sem.at[turn])

    def by_owner(x):
        x = x.reshape(groups, chans, tokens)
        return jnp.concatenate([x[:, :, j * LANES:(j + 1) * LANES] for j in range(tiles)], axis=1).astype(BF16)

    def by_token(x):
        x = x.astype(F32)
        x = jnp.concatenate([x[:, j * chans:(j + 1) * chans, :] for j in range(tiles)], axis=2)
        return x.reshape(ch_rows, tokens)

    fetches[5].wait()
    out_filt[...] = by_owner(filt_ref[...])

    @pl.when(rests)
    def _():
        scatter(0, out_filt, got_filt.at[slot * groups + me], worker, 0)

    @pl.when(works)
    def _():
        scatter(0, out_filt, got_filt.at[me], mc, 1)
        got_filt[me] = out_filt[me]

    for array in range(2):
        pass_on(array)

    def by_share(x):
        x = x.reshape(groups, chans, width)
        return jnp.concatenate([x[:, :, j * LANES:(j + 1) * LANES] for j in range(parts)], axis=1)

    def by_width(x):
        return jnp.concatenate([x[:, j * chans:(j + 1) * chans, :] for j in range(parts)], axis=2).reshape(ch_rows, width)

    def total(ref):
        out = ref[0].astype(F32)
        for p in range(1, ref.shape[0]):
            out = out + ref[p].astype(F32)
        return out.astype(BF16)

    rows = ahead_ref.shape[1]

    def dot(a, b):
        return jnp.dot(a, b, preferred_element_type=F32)

    def lanes(x, s):
        return x[:, s * LANES:(s + 1) * LANES]

    def spectrum(xs):
        first = dot(ahead_ref[...], jnp.concatenate(xs, axis=1))
        tw_re, tw_im = twist_ref[0], twist_ref[1]
        mids = []
        for s in range(half):
            re, im = lanes(first[:rows], s), lanes(first[rows:], s)
            mids.append(jnp.concatenate([re * tw_re - im * tw_im, re * tw_im + im * tw_re], axis=1).astype(BF16))
        out = dot(jnp.concatenate(mids, axis=0), across_ref[...])
        return out[:, :LANES], out[:, LANES:]

    def signal(re, im):
        mid = dot(jnp.concatenate([re, im], axis=1).astype(BF16), return_ref[...])
        tw_re, tw_im = twist_ref[0], twist_ref[1]
        talls = []
        for s in range(half):
            part = mid[s * rows:(s + 1) * rows]
            re, im = part[:, :LANES], part[:, LANES:]
            talls.append(jnp.concatenate([re * tw_re + im * tw_im, im * tw_re - re * tw_im], axis=0).astype(BF16))
        out = dot(back_ref[...], jnp.concatenate(talls, axis=1))
        return [lanes(out, s).reshape(groups, tiles * chans, LANES).astype(BF16) for s in range(half)]

    def slots(x):
        size = x.shape[0] // half
        return [x[s * size:(s + 1) * size] for s in range(half)]

    def stacked(ref):
        return [jnp.concatenate([ref[p, s] for p in range(groups)], axis=0) for s in range(half)]

    def put(ref, xs):
        for s in range(half):
            ref[:, s] = xs[s]

    def put_flat(ref, xs):
        for s in range(half):
            ref[s * groups:(s + 1) * groups] = xs[s]

    def exchange(stage, src, dst):
        scatter(stage, src, dst.at[me], mc, 1)
        dst[me] = src[me]

    def tokens_of(ref):
        return jnp.concatenate([by_token(ref[:, s]) for s in range(half)], axis=0)

    def weight(kind):
        return jnp.concatenate([weights[s, kind] for s in range(half)], axis=0)

    over_first = (((0,), (0,)), ((), ()))
    over_last = (((1,), (1,)), ((), ()))

    @pl.when(works)
    def _():
        take_inner(0)
        for s in range(1, half):
            for kind in range(3):
                weight_copy(kind, s).wait_recv()
        x_in = full_in[...].reshape(width, tokens)
        w_value = weight(0)
        w_gate = weight(1)
        put(out_val, [by_owner(x) for x in slots(dot(w_value, x_in))])
        exchange(1, out_val, got_val)
        gate = dot(w_gate, x_in)

        take_inner(1)
        x_grad = full_grad[...].reshape(width, tokens)
        d_gated = dot(weight(2), x_grad)
        put(out_dif, [by_owner(x) for x in slots(d_gated * gate)])
        exchange(2, out_dif, got_dif)

        for table in tables:
            table.wait()
        took(got_val, groups - 1, seq_recv.at[1])
        v_re, v_im = spectrum(stacked(got_val))
        took(got_filt, half * groups - 1, seq_recv.at[0])
        f_re, f_im = spectrum([
            jnp.concatenate([got_filt[s * groups + p] for p in range(groups)], axis=0) for s in range(half)])
        put(out_mix, signal(f_re * v_re - f_im * v_im, f_re * v_im + f_im * v_re))
        exchange(3, out_mix, got_mix)

        took(got_dif, groups - 1, seq_recv.at[2])
        g_re, g_im = spectrum(stacked(got_dif))
        put(out_dv, signal(f_re * g_re + f_im * g_im, f_re * g_im - f_im * g_re))
        exchange(4, out_dv, got_dv)
        put_flat(out_df, signal(v_re * g_re + v_im * g_im, v_re * g_im - v_im * g_re))
        to_planes(5, out_df, got_df)

        took(got_mix, groups - 1, seq_recv.at[3])
        mixed = tokens_of(got_mix)
        gated_out = (gate * mixed).astype(BF16)
        d_gate = (d_gated * mixed).astype(BF16)
        gate_term = lax.dot_general(d_gate, x_in, over_last, preferred_element_type=F32)
        out_term = lax.dot_general(gated_out, x_grad, over_last, preferred_element_type=F32)
        put_flat(out_w, [
            jnp.concatenate([by_share(a), by_share(b)], axis=1).astype(BF16)
            for a, b in zip(slots(gate_term), slots(out_term))])
        to_planes(6, out_w, got_w)
        from_gate = lax.dot_general(w_gate, d_gate, over_first, preferred_element_type=F32)

        took(got_dv, groups - 1, seq_recv.at[4])
        d_value = tokens_of(got_dv).astype(BF16)
        value_term = lax.dot_general(d_value, x_in, over_last, preferred_element_type=F32)
        put_flat(out_v, [by_share(a).astype(BF16) for a in slots(value_term)])
        to_planes(8, out_v, got_v)
        d_in = lax.dot_general(w_value, d_value, over_first, preferred_element_type=F32) + from_gate
        out_din[...] = d_in.reshape(rings, ch_rows, tokens).astype(BF16)
        outward = [mc - toward * s for s in range(1, half)]
        for block in outward + [other + toward * k for k in reversed(range(half))]:
            send(out_din.at[block], got_din.at[right], (din_send.at[0], din_recv.at[0]), me, block).start()
        got_din[right] = out_din[mc]

    def when_count(semaphore, ref, working, resting):
        @pl.when(works)
        def _():
            took(ref, working, semaphore)

        @pl.when(rests)
        def _():
            took(ref, resting, semaphore)

    when_count(seq_recv.at[6], got_w, groups - 1, groups)
    out_ws[...] = total(got_w)
    spread(7, out_ws, got_ws)
    got_ws[me] = out_ws[...]

    when_count(seq_recv.at[5], got_df, groups - 1, groups)
    dfil_ref[...] = by_token(got_df[...]).astype(BF16)

    when_count(seq_recv.at[8], got_v, groups - 1, groups)
    out_vs[...] = total(got_v)
    spread(9, out_vs, got_vs)
    got_vs[me] = out_vs[...]

    took(got_ws, groups - 1, seq_recv.at[7])
    size = parts * chans
    summed = got_ws[...].astype(F32)
    dw_ref[1] = by_width(summed[:, :size, :]).astype(BF16)
    dw_ref[2] = by_width(summed[:, size:, :]).astype(BF16)
    when_count(din_recv.at[0], got_din, 1, 2)
    din_ref[...] = total(got_din)
    took(got_vs, groups - 1, seq_recv.at[9])
    dw_ref[0] = by_width(got_vs[...].astype(F32)).astype(BF16)

    for array in range(2):
        hop(array, mc, 0).wait_send()
        for k in range(1, half):
            @pl.when(slot < half - k)
            def _():
                hop(array, mc - toward * k, k).wait_send()

    @pl.when(works)
    def _():
        took(out_filt, groups - 1, seq_send.at[0])
        for stage, src in ((1, out_val), (2, out_dif), (3, out_mix), (4, out_dv)):
            took(src, groups - 1, seq_send.at[stage])
        for stage, src in ((5, out_df), (6, out_w), (8, out_v)):
            took(src, half * groups - 1, seq_send.at[stage])
        took(out_din, rings - 1, din_send.at[0])

    @pl.when(rests)
    def _():
        took(out_filt, groups, seq_send.at[0])
        for kind in range(3):
            weight_copy(kind, slot).wait_send()

    took(got_ws, groups - 1, seq_send.at[7])
    took(got_vs, groups - 1, seq_send.at[9])


def finish(scale, din_ref, dw_ref, dfil_ref, din_out, dwv_out, dwg_out, dwo_out, dfil_out):
    din_out[...] = din_ref[...]
    dwv_out[...] = dw_ref[0].astype(F32) * scale
    dwg_out[...] = dw_ref[1].astype(F32) * scale
    dwo_out[...] = dw_ref[2].astype(F32) * scale
    dfil_out[...] = dfil_ref[...].astype(F32) * scale


def solution(mesh):
    groups, rings = mesh.shape["seq"], mesh.shape["ch"]

    def on_device(inputs, w_value, w_gate, w_out, filter_taps, grad_out):
        ch_rows, tokens = inputs.shape
        width = w_value.shape[0]
        chans, tiles, parts = ch_rows // groups, tokens // LANES, width // LANES
        tables = dft_tables(groups * tiles, LANES, chans)
        scale = 1.0 / math.sqrt(tokens * groups)
        vmem = pl.BlockSpec(memory_space=pltpu.VMEM)
        hbm = pl.BlockSpec(memory_space=pltpu.HBM)
        half = rings // 2
        block = pltpu.VMEM((groups, half, tiles * chans, LANES), BF16)
        flat = pltpu.VMEM((half * groups, tiles * chans, LANES), BF16)
        plane = pltpu.VMEM((groups, tiles * chans, LANES), BF16)
        whole = pltpu.VMEM((rings, ch_rows, tokens), BF16)
        share = lambda count: [
            pltpu.VMEM((half * groups, count * parts * chans, LANES), BF16),
            pltpu.VMEM((groups, count * parts * chans, LANES), BF16),
            pltpu.VMEM((count * parts * chans, LANES), BF16),
            pltpu.VMEM((groups, count * parts * chans, LANES), BF16),
        ]
        tokens_out = jax.ShapeDtypeStruct((ch_rows, tokens), F32)
        weight_out = jax.ShapeDtypeStruct((ch_rows, width), F32)
        d_inputs, d_weights, d_filter = pl.pallas_call(
            functools.partial(body, groups, rings),
            out_shape=(
                pltpu.VMEM((ch_rows, tokens), BF16),
                pltpu.VMEM((3, ch_rows, width), BF16),
                pltpu.VMEM((ch_rows, tokens), BF16),
            ),
            in_specs=[hbm] * 11,
            out_specs=(vmem,) * 3,
            scratch_shapes=[
                whole, whole, pltpu.VMEM((ch_rows, tokens), F32), pltpu.VMEM((half, 3, ch_rows, width), BF16),
                plane, flat] + [block] * 8 + [flat, plane]
            + [whole, pltpu.VMEM((2, ch_rows, tokens), BF16)] + share(2) + share(1)
            + [pltpu.VMEM(table.shape, table.dtype) for table in tables] + [
                pltpu.SemaphoreType.DMA((10,)),
                pltpu.SemaphoreType.DMA((10,)),
                pltpu.SemaphoreType.DMA((1,)),
                pltpu.SemaphoreType.DMA((1,)),
                pltpu.SemaphoreType.DMA((2, half)),
                pltpu.SemaphoreType.DMA((2, rings)),
                pltpu.SemaphoreType.DMA((3,)),
                pltpu.SemaphoreType.DMA((half, 3)),
                pltpu.SemaphoreType.DMA((5,)),
                pltpu.SemaphoreType.DMA((6,)),
                pltpu.SemaphoreType.REGULAR((len(near(groups)) + half - 2,)),
            ],
            compiler_params=pltpu.CompilerParams(collective_id=0, has_side_effects=True),
        )(
            inputs, w_value.T, w_gate.T, w_out, filter_taps, grad_out, *tables,
        )
        d_inputs, d_w_value, d_w_gate, d_w_out, d_filter = pl.pallas_call(
            functools.partial(finish, scale),
            out_shape=(
                jax.ShapeDtypeStruct((ch_rows, tokens), BF16), weight_out, weight_out, weight_out, tokens_out,
            ),
            in_specs=[vmem] * 3,
            out_specs=(vmem,) * 5,
            compiler_params=pltpu.CompilerParams(vmem_limit_bytes=8 << 20),
        )(d_inputs, d_weights, d_filter)
        return d_inputs, d_w_value.T, d_w_gate.T, d_w_out, d_filter

    return jax.shard_map(
        on_device,
        mesh=mesh,
        in_specs=(P("ch", "seq"), P(None, "ch"), P(None, "ch"), P("ch", None), P("ch", "seq"), P("ch", "seq")),
        out_specs=(P("ch", "seq"), P(None, "ch"), P(None, "ch"), P("ch", None), P("ch", "seq")),
        check_vma=False,
    )
```

time: 31.8 us -> 33.3 us (1.047)
  Pallas kernels: 31 us -> 32.5 us
    pallas_call x1, Pallas kernels: 30.3 us -> 31.8 us  [on_device(): pl.pallas_call(functools.partial(body, groups, rings), out_shape=(pltpu.V...]
where the time goes in v2:
time: 33.3 us; the launch traced here: 33.2 us
  Pallas kernels  32.5 us (98%)
  between operations  0.64 us (2%)
    pallas_call x1, Pallas kernels, on_device(): pl.pallas_call(functools.partial(body, groups, rings), out_shape=(pltpu.V...  31.8 us
    pallas_call x1, Pallas kernels, on_device(): pl.pallas_call(functools.partial(finish, scale), out_shape=(jax.ShapeDtyp...  0.76 us

profile of v2, /device:TPU:0, one launch (start us, length us, event | category | flops | bytes accessed | tf_op | source)
XLA Modules:
  0.0 33.2 jit_solution(12996585225427403225)
XLA Ops:
  0.6 31.8 %shard_map.146 = (bf16[64,512]{1,0:T(8,128)(2,1)S(1)}, bf16[3,64,256]{2,1,0:T(8,128)(2,1)S(1)}, bf16[64,512]{1,0:T(8,128)(2,1)S(1)}) custom-call(bf16[64,512]{1,0:T(8,128)(2,1)} %in_hbm.1, bf16[64,256]{1,0:T(8,128)(2,1)} %bitcast.4, bf16[64,256]{1,0:T(8,128)(2,1)} %bitcast.5, bf16[64,256]{1,0:T(8,128)(2,1)} %wo_hbm.1, f32[64,512]{1,0:T(8,128)} %filt_hbm.1, ...), custom_call_target="tpu_custom_call" | custom-call | tf_op jit(solution)/shard_map/pallas_call | solution.py:436
  32.4 0.8 %shard_map.147 = (bf16[64,512]{1,0:T(8,128)(2,1)}, f32[64,256]{1,0:T(8,128)}, f32[64,256]{1,0:T(8,128)}, f32[64,256]{1,0:T(8,128)}, f32[64,512]{1,0:T(8,128)}) custom-call(bf16[64,512]{1,0:T(8,128)(2,1)S(1)} %get-tuple-element.13.din_ref, bf16[3,64,256]{2,1,0:T(8,128)(2,1)S(1)} %get-tuple-element.14.dw_ref, bf16[64,512]{1,0:T(8,128)(2,1)S(1)} %get-tuple-element.15.dfil_ref), custom_call_target="tpu_custom_call" | custom-call | tf_op jit(solution)/shard_map/pallas_call | solution.py:466

commit v3 on v2

--- a/solution.py
+++ b/solution.py
@@ -56,9 +56,9 @@
     din_ref, dw_ref, dfil_ref,
     full_in, full_grad, filt_ref, weights, out_filt, got_filt, out_val, got_val, out_dif, got_dif,
     out_mix, got_mix, out_dv, got_dv, out_df, got_df,
-    out_din, got_din, out_w, got_w, out_ws, got_ws, out_v, got_v, out_vs, got_vs,
+    out_din, got_din, out_w, got_w, out_ws, got_ws, out_v, got_v,
     ahead_ref, back_ref, across_ref, return_ref, twist_ref,
-    seq_send, seq_recv, din_send, din_recv, line_send, line_recv, weight_send, weight_recv,
+    seq_send, seq_recv, din_send, din_recv, line_send, line_recv, share_send, share_recv,
     table_sem, fetch_sem, round_sem,
 ):
     me = lax.axis_index("seq")
@@ -69,6 +69,7 @@
     width = full_in.shape[0] * ch_rows
     parts = width // LANES
     half = rings // 2
+    splits = weights.shape[1]
     right = lax.div(mc, half)
     toward = 1 - 2 * right
     worker = half - 1 + right
@@ -107,7 +108,7 @@
         pltpu.make_async_copy(src, dst, fetch_sem.at[i])
         for i, (src, dst) in enumerate((
             (in_hbm, full_in.at[mc]), (grad_hbm, full_grad.at[mc]),
-            (wv_hbm, weights.at[0, 0]), (wg_hbm, weights.at[0, 1]), (wo_hbm, weights.at[0, 2]),
+            (wv_hbm, weights.at[0, :, 0]), (wg_hbm, weights.at[0, :, 1]), (wo_hbm, weights.at[0, :, 2]),
             (filt_hbm, filt_ref)))
     ]
     tables = [
@@ -154,40 +155,68 @@
             scatter(stage, src, dst.at[me], mc - toward * s, 1 if s == 0 else 0, s * groups)
         dst[me] = src[me]
 
+    def to_owners(stage, src, dst):
+        for s in range(1, half):
+            each(groups, lambda k: send(
+                src.at[seq_peer(k), s], dst.at[me, 0], stage_sems(stage), seq_peer(k), mc - toward * s).start())
+
     wholes = (full_in, full_grad)
 
-    def hop(array, block, k):
+    def block_to(array, block, ch, k):
         return send(
             wholes[array].at[block], wholes[array].at[block],
-            (line_send.at[array, k], line_recv.at[array, block]), me, mc + toward)
+            (line_send.at[array, k], line_recv.at[array, block]), me, ch)
+
+    def take(array):
+        for k in range(1, rings):
+            block_to(array, lax.rem(mc + k, rings), mc, 0).wait_recv()
 
     def pass_on(array):
-        for k in range(1, half):
-            @pl.when(slot < half - k)
-            def _():
-                hop(array, mc - toward * k, k).wait_recv()
-                hop(array, mc - toward * k, k).start()
-
-    def take_inner(array):
-        for k in range(half):
-            hop(array, other + toward * k, 0).wait_recv()
-
-    def weight_copy(kind, s):
-        return send(weights.at[0, kind], weights.at[s, kind], (weight_send.at[kind], weight_recv.at[s, kind]), me, worker)
+        for s in range(1, half):
+            inner = [mc - toward * t for t in range(1, half) if t != s]
+            for block in [other + toward * k for k in range(half)] + inner:
+                block_to(array, block, mc - toward * s, 1).start()
+
+    mine = lax.rem(me, splits)
+
+    def share_up(s):
+        return send(weights.at[0, mine], weights.at[s, mine], (share_send.at[0], share_recv.at[s, 0]), me, worker)
+
+    def share_across(s, k):
+        return send(
+            weights.at[s, mine], weights.at[s, mine], (share_send.at[s], share_recv.at[s, 1]), me ^ k, mc)
+
+    for kind in range(3):
+        fetches[2 + kind].wait()
+
+    @pl.when(rests)
+    def _():
+        share_up(slot).start()
 
     for array in range(2):
         fetches[array].wait()
-        hop(array, mc, 0).start()
-    for kind in range(3):
-        fetches[2 + kind].wait()
+
+        @pl.when(works)
+        def _():
+            block_to(array, mc, other, 0).start()
 
         @pl.when(rests)
         def _():
-            weight_copy(kind, slot).start()
+            block_to(array, mc, worker, 1).start()
 
     for turn in range(len(hops) + half - 2):
         greet(round_sem.at[turn])
         greeted(round_sem.at[turn])
+        if turn == half - 2:
+            for array in range(2):
+                @pl.when(works)
+                def _():
+                    for s in range(1, half):
+                        block_to(array, mc, mc - toward * s, 1).start()
+
+                @pl.when(rests)
+                def _():
+                    block_to(array, mc, other, 0).start()
 
     def by_owner(x):
         x = x.reshape(groups, chans, tokens)
@@ -210,8 +239,12 @@
         scatter(0, out_filt, got_filt.at[me], mc, 1)
         got_filt[me] = out_filt[me]
 
-    for array in range(2):
-        pass_on(array)
+    @pl.when(works)
+    def _():
+        for s in range(1, half):
+            share_up(s).wait_recv()
+            for k in range(1, splits):
+                share_across(s, k).start()
 
     def by_share(x):
         x = x.reshape(groups, chans, width)
@@ -274,33 +307,47 @@
         scatter(stage, src, dst.at[me], mc, 1)
         dst[me] = src[me]
 
-    def tokens_of(ref):
-        return jnp.concatenate([by_token(ref[:, s]) for s in range(half)], axis=0)
-
-    def weight(kind):
-        return jnp.concatenate([weights[s, kind] for s in range(half)], axis=0)
+    def tokens_of(ref, count):
+        return jnp.concatenate([by_token(ref[:, s]) for s in range(count)], axis=0)
+
+    def weight(kind, count):
+        return jnp.concatenate([weights[s, q, kind] for s in range(count) for q in range(splits)], axis=0)
+
+    def reduce_weights(gate, d_gated, d_gate, mixed, x_in, x_grad):
+        gated_out = (gate[:ch_rows] * mixed[:ch_rows]).astype(BF16)
+        gate_term = lax.dot_general(d_gate[:ch_rows], x_in, over_last, preferred_element_type=F32)
+        out_term = lax.dot_general(gated_out, x_grad, over_last, preferred_element_type=F32)
+        out_w[...] = jnp.concatenate([by_share(gate_term), by_share(out_term)], axis=1).astype(BF16)
+        exchange(6, out_w, got_w)
+
+    def reduce_value(d_value, x_in):
+        value_term = lax.dot_general(d_value[:ch_rows], x_in, over_last, preferred_element_type=F32)
+        out_v[...] = value_term.astype(BF16)
+        spread(8, out_v, got_v)
 
     over_first = (((0,), (0,)), ((), ()))
     over_last = (((1,), (1,)), ((), ()))
 
     @pl.when(works)
     def _():
-        take_inner(0)
+        take(0)
         for s in range(1, half):
-            for kind in range(3):
-                weight_copy(kind, s).wait_recv()
+            across = weights.at[s, pl.ds(0, splits - 1)]
+            pltpu.make_async_copy(across, across, share_recv.at[s, 1]).wait()
         x_in = full_in[...].reshape(width, tokens)
-        w_value = weight(0)
-        w_gate = weight(1)
+        w_value = weight(0, half)
+        w_gate = weight(1, half)
         put(out_val, [by_owner(x) for x in slots(dot(w_value, x_in))])
         exchange(1, out_val, got_val)
+        pass_on(0)
         gate = dot(w_gate, x_in)
 
-        take_inner(1)
+        take(1)
         x_grad = full_grad[...].reshape(width, tokens)
-        d_gated = dot(weight(2), x_grad)
+        d_gated = dot(weight(2, half), x_grad)
         put(out_dif, [by_owner(x) for x in slots(d_gated * gate)])
         exchange(2, out_dif, got_dif)
+        pass_on(1)
 
         for table in tables:
             table.wait()
@@ -310,32 +357,26 @@
         f_re, f_im = spectrum([
             jnp.concatenate([got_filt[s * groups + p] for p in range(groups)], axis=0) for s in range(half)])
         put(out_mix, signal(f_re * v_re - f_im * v_im, f_re * v_im + f_im * v_re))
+        to_owners(10, out_mix, got_mix)
         exchange(3, out_mix, got_mix)
 
         took(got_dif, groups - 1, seq_recv.at[2])
         g_re, g_im = spectrum(stacked(got_dif))
         put(out_dv, signal(f_re * g_re + f_im * g_im, f_re * g_im - f_im * g_re))
+        to_owners(11, out_dv, got_dv)
         exchange(4, out_dv, got_dv)
         put_flat(out_df, signal(v_re * g_re + v_im * g_im, v_re * g_im - v_im * g_re))
         to_planes(5, out_df, got_df)
 
         took(got_mix, groups - 1, seq_recv.at[3])
-        mixed = tokens_of(got_mix)
-        gated_out = (gate * mixed).astype(BF16)
+        mixed = tokens_of(got_mix, half)
         d_gate = (d_gated * mixed).astype(BF16)
-        gate_term = lax.dot_general(d_gate, x_in, over_last, preferred_element_type=F32)
-        out_term = lax.dot_general(gated_out, x_grad, over_last, preferred_element_type=F32)
-        put_flat(out_w, [
-            jnp.concatenate([by_share(a), by_share(b)], axis=1).astype(BF16)
-            for a, b in zip(slots(gate_term), slots(out_term))])
-        to_planes(6, out_w, got_w)
+        reduce_weights(gate, d_gated, d_gate, mixed, x_in, x_grad)
         from_gate = lax.dot_general(w_gate, d_gate, over_first, preferred_element_type=F32)
 
         took(got_dv, groups - 1, seq_recv.at[4])
-        d_value = tokens_of(got_dv).astype(BF16)
-        value_term = lax.dot_general(d_value, x_in, over_last, preferred_element_type=F32)
-        put_flat(out_v, [by_share(a).astype(BF16) for a in slots(value_term)])
-        to_planes(8, out_v, got_v)
+        d_value = tokens_of(got_dv, half).astype(BF16)
+        reduce_value(d_value, x_in)
         d_in = lax.dot_general(w_value, d_value, over_first, preferred_element_type=F32) + from_gate
         out_din[...] = d_in.reshape(rings, ch_rows, tokens).astype(BF16)
         outward = [mc - toward * s for s in range(1, half)]
@@ -343,6 +384,21 @@
             send(out_din.at[block], got_din.at[right], (din_send.at[0], din_recv.at[0]), me, block).start()
         got_din[right] = out_din[mc]
 
+    @pl.when(rests)
+    def _():
+        take(0)
+        x_in = full_in[...].reshape(width, tokens)
+        gate = dot(weight(1, 1), x_in)
+        take(1)
+        x_grad = full_grad[...].reshape(width, tokens)
+        d_gated = dot(weight(2, 1), x_grad)
+        took(got_mix, groups // half, seq_recv.at[10])
+        mixed = tokens_of(got_mix, 1)
+        d_gate = (d_gated * mixed).astype(BF16)
+        reduce_weights(gate, d_gated, d_gate, mixed, x_in, x_grad)
+        took(got_dv, groups // half, seq_recv.at[11])
+        reduce_value(tokens_of(got_dv, 1).astype(BF16), x_in)
+
     def when_count(semaphore, ref, working, resting):
         @pl.when(works)
         def _():
@@ -352,53 +408,56 @@
         def _():
             took(ref, resting, semaphore)
 
-    when_count(seq_recv.at[6], got_w, groups - 1, groups)
+    took(got_w, groups - 1, seq_recv.at[6])
     out_ws[...] = total(got_w)
     spread(7, out_ws, got_ws)
     got_ws[me] = out_ws[...]
+    got_v[me] = out_v[...]
 
     when_count(seq_recv.at[5], got_df, groups - 1, groups)
     dfil_ref[...] = by_token(got_df[...]).astype(BF16)
 
-    when_count(seq_recv.at[8], got_v, groups - 1, groups)
-    out_vs[...] = total(got_v)
-    spread(9, out_vs, got_vs)
-    got_vs[me] = out_vs[...]
-
+    took(got_v, groups - 1, seq_recv.at[8])
+    dw_ref[0] = total(got_v)
+    when_count(din_recv.at[0], got_din, 1, 2)
+    din_ref[...] = total(got_din)
     took(got_ws, groups - 1, seq_recv.at[7])
     size = parts * chans
     summed = got_ws[...].astype(F32)
     dw_ref[1] = by_width(summed[:, :size, :]).astype(BF16)
     dw_ref[2] = by_width(summed[:, size:, :]).astype(BF16)
-    when_count(din_recv.at[0], got_din, 1, 2)
-    din_ref[...] = total(got_din)
-    took(got_vs, groups - 1, seq_recv.at[9])
-    dw_ref[0] = by_width(got_vs[...].astype(F32)).astype(BF16)
 
     for array in range(2):
-        hop(array, mc, 0).wait_send()
-        for k in range(1, half):
-            @pl.when(slot < half - k)
-            def _():
-                hop(array, mc - toward * k, k).wait_send()
+        block_to(array, mc, other, 0).wait_send()
+
+        @pl.when(works)
+        def _():
+            for s in range(1, half):
+                took(wholes[array], rings - 1, line_send.at[array, 1])
+
+        @pl.when(rests)
+        def _():
+            block_to(array, mc, worker, 1).wait_send()
 
     @pl.when(works)
     def _():
         took(out_filt, groups - 1, seq_send.at[0])
         for stage, src in ((1, out_val), (2, out_dif), (3, out_mix), (4, out_dv)):
             took(src, groups - 1, seq_send.at[stage])
-        for stage, src in ((5, out_df), (6, out_w), (8, out_v)):
-            took(src, half * groups - 1, seq_send.at[stage])
+        for stage, src in ((10, out_mix), (11, out_dv)):
+            took(src, (half - 1) * groups // half, seq_send.at[stage])
+        took(out_df, half * groups - 1, seq_send.at[5])
         took(out_din, rings - 1, din_send.at[0])
+        for s in range(1, half):
+            took(weights.at[s], splits - 1, share_send.at[s])
 
     @pl.when(rests)
     def _():
         took(out_filt, groups, seq_send.at[0])
-        for kind in range(3):
-            weight_copy(kind, slot).wait_send()
-
-    took(got_ws, groups - 1, seq_send.at[7])
-    took(got_vs, groups - 1, seq_send.at[9])
+        share_up(slot).wait_send()
+
+    for stage, src in ((6, got_w), (7, got_ws), (8, got_v)):
+        took(src, groups - 1, seq_send.at[stage])
 
 
 def finish(scale, din_ref, dw_ref, dfil_ref, din_out, dwv_out, dwg_out, dwo_out, dfil_out):
@@ -425,12 +484,10 @@
         flat = pltpu.VMEM((half * groups, tiles * chans, LANES), BF16)
         plane = pltpu.VMEM((groups, tiles * chans, LANES), BF16)
         whole = pltpu.VMEM((rings, ch_rows, tokens), BF16)
-        share = lambda count: [
-            pltpu.VMEM((half * groups, count * parts * chans, LANES), BF16),
-            pltpu.VMEM((groups, count * parts * chans, LANES), BF16),
-            pltpu.VMEM((count * parts * chans, LANES), BF16),
-            pltpu.VMEM((groups, count * parts * chans, LANES), BF16),
-        ]
+        splits = min(groups, ch_rows // 16)
+        split = lambda w: w.reshape(splits, ch_rows // splits, width)
+        share = pltpu.VMEM((groups, 2 * parts * chans, LANES), BF16)
+        rows_of = pltpu.VMEM((ch_rows, width), BF16)
         tokens_out = jax.ShapeDtypeStruct((ch_rows, tokens), F32)
         weight_out = jax.ShapeDtypeStruct((ch_rows, width), F32)
         d_inputs, d_weights, d_filter = pl.pallas_call(
@@ -443,25 +500,26 @@
             in_specs=[hbm] * 11,
             out_specs=(vmem,) * 3,
             scratch_shapes=[
-                whole, whole, pltpu.VMEM((ch_rows, tokens), F32), pltpu.VMEM((half, 3, ch_rows, width), BF16),
+                whole, whole, pltpu.VMEM((ch_rows, tokens), F32), pltpu.VMEM((half, splits, 3, ch_rows // splits, width), BF16),
                 plane, flat] + [block] * 8 + [flat, plane]
-            + [whole, pltpu.VMEM((2, ch_rows, tokens), BF16)] + share(2) + share(1)
+            + [whole, pltpu.VMEM((2, ch_rows, tokens), BF16)]
+            + [share, share, pltpu.VMEM((2 * parts * chans, LANES), BF16), share, rows_of, pltpu.VMEM((groups, ch_rows, width), BF16)]
             + [pltpu.VMEM(table.shape, table.dtype) for table in tables] + [
-                pltpu.SemaphoreType.DMA((10,)),
-                pltpu.SemaphoreType.DMA((10,)),
+                pltpu.SemaphoreType.DMA((12,)),
+                pltpu.SemaphoreType.DMA((12,)),
                 pltpu.SemaphoreType.DMA((1,)),
                 pltpu.SemaphoreType.DMA((1,)),
-                pltpu.SemaphoreType.DMA((2, half)),
+                pltpu.SemaphoreType.DMA((2, 2)),
                 pltpu.SemaphoreType.DMA((2, rings)),
-                pltpu.SemaphoreType.DMA((3,)),
-                pltpu.SemaphoreType.DMA((half, 3)),
+                pltpu.SemaphoreType.DMA((half,)),
+                pltpu.SemaphoreType.DMA((half, 2)),
                 pltpu.SemaphoreType.DMA((5,)),
                 pltpu.SemaphoreType.DMA((6,)),
                 pltpu.SemaphoreType.REGULAR((len(near(groups)) + half - 2,)),
             ],
             compiler_params=pltpu.CompilerParams(collective_id=0, has_side_effects=True),
         )(
-            inputs, w_value.T, w_gate.T, w_out, filter_taps, grad_out, *tables,
+            inputs, split(w_value.T), split(w_gate.T), split(w_out), filter_taps, grad_out, *tables,
         )
         d_inputs, d_w_value, d_w_gate, d_w_out, d_filter = pl.pallas_call(
             functools.partial(finish, scale),

time: 33.3 us -> 31.7 us (0.952)
  Pallas kernels: 32.5 us -> 30.9 us
    pallas_call x1, Pallas kernels: 31.8 us -> 30.2 us  [on_device(): pl.pallas_call(functools.partial(body, groups, rings), out_shape=(pltpu.V...]
where the time goes in v3:
time: 31.7 us; the launch traced here: 31.6 us
  Pallas kernels  30.9 us (97%)
  between operations  0.64 us (2%)
    pallas_call x1, Pallas kernels, on_device(): pl.pallas_call(functools.partial(body, groups, rings), out_shape=(pltpu.V...  30.2 us
    pallas_call x1, Pallas kernels, on_device(): pl.pallas_call(functools.partial(finish, scale), out_shape=(jax.ShapeDtyp...  0.76 us

profile of v3, /device:TPU:0, one launch (start us, length us, event | category | flops | bytes accessed | tf_op | source)
XLA Modules:
  0.0 31.6 jit_solution(10983259398858306417)
XLA Ops:
  0.6 30.2 %shard_map.146 = (bf16[64,512]{1,0:T(8,128)(2,1)S(1)}, bf16[3,64,256]{2,1,0:T(8,128)(2,1)S(1)}, bf16[64,512]{1,0:T(8,128)(2,1)S(1)}) custom-call(bf16[64,512]{1,0:T(8,128)(2,1)} %in_hbm.1, bf16[4,16,256]{2,1,0:T(8,128)(2,1)} %bitcast.9, bf16[4,16,256]{2,1,0:T(8,128)(2,1)} %bitcast.10, bf16[4,16,256]{2,1,0:T(8,128)(2,1)} %bitcast.11, f32[64,512]{1,0:T(8,128)} %filt_hbm.1, ...), custom_call_target="tpu_custom_call" | custom-call | tf_op jit(solution)/shard_map/pallas_call | solution.py:493
  30.8 0.8 %shard_map.147 = (bf16[64,512]{1,0:T(8,128)(2,1)}, f32[64,256]{1,0:T(8,128)}, f32[64,256]{1,0:T(8,128)}, f32[64,256]{1,0:T(8,128)}, f32[64,512]{1,0:T(8,128)}) custom-call(bf16[64,512]{1,0:T(8,128)(2,1)S(1)} %get-tuple-element.13.din_ref, bf16[3,64,256]{2,1,0:T(8,128)(2,1)S(1)} %get-tuple-element.14.dw_ref, bf16[64,512]{1,0:T(8,128)(2,1)S(1)} %get-tuple-element.15.dfil_ref), custom_call_target="tpu_custom_call" | custom-call | tf_op jit(solution)/shard_map/pallas_call | solution.py:524

commit v4 on v3

--- a/solution.py
+++ b/solution.py
@@ -56,7 +56,7 @@
     din_ref, dw_ref, dfil_ref,
     full_in, full_grad, filt_ref, weights, out_filt, got_filt, out_val, got_val, out_dif, got_dif,
     out_mix, got_mix, out_dv, got_dv, out_df, got_df,
-    out_din, got_din, out_w, got_w, out_ws, got_ws, out_v, got_v,
+    out_din, got_din, out_w, got_w, out_ws, got_ws, out_v, got_v, gate_ref, gated_ref,
     ahead_ref, back_ref, across_ref, return_ref, twist_ref,
     seq_send, seq_recv, din_send, din_recv, line_send, line_recv, share_send, share_recv,
     table_sem, fetch_sem, round_sem,
@@ -120,10 +120,8 @@
     for copy in fetches:
         copy.start()
 
-    @pl.when(works)
-    def _():
-        for copy in tables:
-            copy.start()
+    for copy in tables:
+        copy.start()
 
     greeted(barrier)
 
@@ -155,11 +153,6 @@
             scatter(stage, src, dst.at[me], mc - toward * s, 1 if s == 0 else 0, s * groups)
         dst[me] = src[me]
 
-    def to_owners(stage, src, dst):
-        for s in range(1, half):
-            each(groups, lambda k: send(
-                src.at[seq_peer(k), s], dst.at[me, 0], stage_sems(stage), seq_peer(k), mc - toward * s).start())
-
     wholes = (full_in, full_grad)
 
     def block_to(array, block, ch, k):
@@ -167,15 +160,22 @@
             wholes[array].at[block], wholes[array].at[block],
             (line_send.at[array, k], line_recv.at[array, block]), me, ch)
 
-    def take(array):
-        for k in range(1, rings):
-            block_to(array, lax.rem(mc + k, rings), mc, 0).wait_recv()
-
-    def pass_on(array):
+    def take(array, blocks):
+        for block in blocks:
+            block_to(array, block, mc, 0).wait_recv()
+
+    def pass_on(array, block):
         for s in range(1, half):
-            inner = [mc - toward * t for t in range(1, half) if t != s]
-            for block in [other + toward * k for k in range(half)] + inner:
-                block_to(array, block, mc - toward * s, 1).start()
+            block_to(array, block, mc - toward * s, 1).start()
+
+    def pass_inner(array):
+        for s in range(1, half):
+            for t in range(1, half):
+                if t != s:
+                    block_to(array, mc - toward * t, mc - toward * s, 1).start()
+
+    far_blocks = [other + toward * k for k in range(1, half)]
+    outer_blocks = [mc - toward * k for k in range(1, half)]
 
     mine = lax.rem(me, splits)
 
@@ -230,14 +230,8 @@
     fetches[5].wait()
     out_filt[...] = by_owner(filt_ref[...])
 
-    @pl.when(rests)
-    def _():
-        scatter(0, out_filt, got_filt.at[slot * groups + me], worker, 0)
-
-    @pl.when(works)
-    def _():
-        scatter(0, out_filt, got_filt.at[me], mc, 1)
-        got_filt[me] = out_filt[me]
+    scatter(0, out_filt, got_filt.at[me], mc, 1)
+    got_filt[me] = out_filt[me]
 
     @pl.when(works)
     def _():
@@ -264,40 +258,27 @@
     def dot(a, b):
         return jnp.dot(a, b, preferred_element_type=F32)
 
-    def lanes(x, s):
-        return x[:, s * LANES:(s + 1) * LANES]
-
-    def spectrum(xs):
-        first = dot(ahead_ref[...], jnp.concatenate(xs, axis=1))
+    def spectrum(x):
+        first = dot(ahead_ref[...], x)
+        re, im = first[:rows], first[rows:]
         tw_re, tw_im = twist_ref[0], twist_ref[1]
-        mids = []
-        for s in range(half):
-            re, im = lanes(first[:rows], s), lanes(first[rows:], s)
-            mids.append(jnp.concatenate([re * tw_re - im * tw_im, re * tw_im + im * tw_re], axis=1).astype(BF16))
-        out = dot(jnp.concatenate(mids, axis=0), across_ref[...])
+        mid = jnp.concatenate([re * tw_re - im * tw_im, re * tw_im + im * tw_re], axis=1).astype(BF16)
+        out = dot(mid, across_ref[...])
         return out[:, :LANES], out[:, LANES:]
 
     def signal(re, im):
         mid = dot(jnp.concatenate([re, im], axis=1).astype(BF16), return_ref[...])
+        re, im = mid[:, :LANES], mid[:, LANES:]
         tw_re, tw_im = twist_ref[0], twist_ref[1]
-        talls = []
-        for s in range(half):
-            part = mid[s * rows:(s + 1) * rows]
-            re, im = part[:, :LANES], part[:, LANES:]
-            talls.append(jnp.concatenate([re * tw_re + im * tw_im, im * tw_re - re * tw_im], axis=0).astype(BF16))
-        out = dot(back_ref[...], jnp.concatenate(talls, axis=1))
-        return [lanes(out, s).reshape(groups, tiles * chans, LANES).astype(BF16) for s in range(half)]
+        tall = jnp.concatenate([re * tw_re + im * tw_im, im * tw_re - re * tw_im], axis=0).astype(BF16)
+        return dot(back_ref[...], tall).reshape(groups, tiles * chans, LANES).astype(BF16)
 
     def slots(x):
         size = x.shape[0] // half
         return [x[s * size:(s + 1) * size] for s in range(half)]
 
     def stacked(ref):
-        return [jnp.concatenate([ref[p, s] for p in range(groups)], axis=0) for s in range(half)]
-
-    def put(ref, xs):
-        for s in range(half):
-            ref[:, s] = xs[s]
+        return jnp.concatenate([ref[p] for p in range(groups)], axis=0)
 
     def put_flat(ref, xs):
         for s in range(half):
@@ -306,9 +287,6 @@
     def exchange(stage, src, dst):
         scatter(stage, src, dst.at[me], mc, 1)
         dst[me] = src[me]
-
-    def tokens_of(ref, count):
-        return jnp.concatenate([by_token(ref[:, s]) for s in range(count)], axis=0)
 
     def weight(kind, count):
         return jnp.concatenate([weights[s, q, kind] for s in range(count) for q in range(splits)], axis=0)
@@ -328,85 +306,82 @@
     over_first = (((0,), (0,)), ((), ()))
     over_last = (((1,), (1,)), ((), ()))
 
+    def when_count(semaphore, ref, working, resting):
+        @pl.when(works)
+        def _():
+            took(ref, working, semaphore)
+
+        @pl.when(rests)
+        def _():
+            took(ref, resting, semaphore)
+
     @pl.when(works)
     def _():
-        take(0)
+        for array in range(2):
+            take(array, [other])
+            pass_on(array, other)
+        take(0, outer_blocks + far_blocks)
         for s in range(1, half):
             across = weights.at[s, pl.ds(0, splits - 1)]
             pltpu.make_async_copy(across, across, share_recv.at[s, 1]).wait()
         x_in = full_in[...].reshape(width, tokens)
-        w_value = weight(0, half)
-        w_gate = weight(1, half)
-        put(out_val, [by_owner(x) for x in slots(dot(w_value, x_in))])
-        exchange(1, out_val, got_val)
-        pass_on(0)
-        gate = dot(w_gate, x_in)
-
-        take(1)
+        put_flat(out_val, [by_owner(x) for x in slots(dot(weight(0, half), x_in))])
+        to_planes(1, out_val, got_val)
+        gate = dot(weight(1, half), x_in)
+        gate_ref[...] = gate[:ch_rows]
+        take(1, outer_blocks + far_blocks)
         x_grad = full_grad[...].reshape(width, tokens)
         d_gated = dot(weight(2, half), x_grad)
-        put(out_dif, [by_owner(x) for x in slots(d_gated * gate)])
-        exchange(2, out_dif, got_dif)
-        pass_on(1)
-
-        for table in tables:
-            table.wait()
-        took(got_val, groups - 1, seq_recv.at[1])
-        v_re, v_im = spectrum(stacked(got_val))
-        took(got_filt, half * groups - 1, seq_recv.at[0])
-        f_re, f_im = spectrum([
-            jnp.concatenate([got_filt[s * groups + p] for p in range(groups)], axis=0) for s in range(half)])
-        put(out_mix, signal(f_re * v_re - f_im * v_im, f_re * v_im + f_im * v_re))
-        to_owners(10, out_mix, got_mix)
-        exchange(3, out_mix, got_mix)
-
-        took(got_dif, groups - 1, seq_recv.at[2])
-        g_re, g_im = spectrum(stacked(got_dif))
-        put(out_dv, signal(f_re * g_re + f_im * g_im, f_re * g_im - f_im * g_re))
-        to_owners(11, out_dv, got_dv)
-        exchange(4, out_dv, got_dv)
-        put_flat(out_df, signal(v_re * g_re + v_im * g_im, v_re * g_im - v_im * g_re))
-        to_planes(5, out_df, got_df)
-
-        took(got_mix, groups - 1, seq_recv.at[3])
-        mixed = tokens_of(got_mix, half)
-        d_gate = (d_gated * mixed).astype(BF16)
-        reduce_weights(gate, d_gated, d_gate, mixed, x_in, x_grad)
-        from_gate = lax.dot_general(w_gate, d_gate, over_first, preferred_element_type=F32)
-
-        took(got_dv, groups - 1, seq_recv.at[4])
-        d_value = tokens_of(got_dv, half).astype(BF16)
-        reduce_value(d_value, x_in)
-        d_in = lax.dot_general(w_value, d_value, over_first, preferred_element_type=F32) + from_gate
-        out_din[...] = d_in.reshape(rings, ch_rows, tokens).astype(BF16)
-        outward = [mc - toward * s for s in range(1, half)]
-        for block in outward + [other + toward * k for k in reversed(range(half))]:
-            send(out_din.at[block], got_din.at[right], (din_send.at[0], din_recv.at[0]), me, block).start()
-        got_din[right] = out_din[mc]
+        put_flat(out_dif, [by_owner(x) for x in slots(d_gated * gate)])
+        to_planes(2, out_dif, got_dif)
+        gated_ref[...] = d_gated[:ch_rows]
+        for array in range(2):
+            for block in far_blocks:
+                pass_on(array, block)
+            pass_inner(array)
+
+    for table in tables:
+        table.wait()
+    took(got_filt, groups - 1, seq_recv.at[0])
+    f_re, f_im = spectrum(stacked(got_filt))
+    when_count(seq_recv.at[1], got_val, groups - 1, groups)
+    v_re, v_im = spectrum(stacked(got_val))
+    out_mix[...] = signal(f_re * v_re - f_im * v_im, f_re * v_im + f_im * v_re)
+    exchange(3, out_mix, got_mix)
+
+    when_count(seq_recv.at[2], got_dif, groups - 1, groups)
+    g_re, g_im = spectrum(stacked(got_dif))
+    out_dv[...] = signal(f_re * g_re + f_im * g_im, f_re * g_im - f_im * g_re)
+    exchange(4, out_dv, got_dv)
+    out_df[...] = signal(v_re * g_re + v_im * g_im, v_re * g_im - v_im * g_re)
+    exchange(5, out_df, got_df)
 
     @pl.when(rests)
     def _():
-        take(0)
-        x_in = full_in[...].reshape(width, tokens)
-        gate = dot(weight(1, 1), x_in)
-        take(1)
-        x_grad = full_grad[...].reshape(width, tokens)
-        d_gated = dot(weight(2, 1), x_grad)
-        took(got_mix, groups // half, seq_recv.at[10])
-        mixed = tokens_of(got_mix, 1)
-        d_gate = (d_gated * mixed).astype(BF16)
-        reduce_weights(gate, d_gated, d_gate, mixed, x_in, x_grad)
-        took(got_dv, groups // half, seq_recv.at[11])
-        reduce_value(tokens_of(got_dv, 1).astype(BF16), x_in)
-
-    def when_count(semaphore, ref, working, resting):
-        @pl.when(works)
-        def _():
-            took(ref, working, semaphore)
-
-        @pl.when(rests)
-        def _():
-            took(ref, resting, semaphore)
+        take(0, [lax.rem(mc + k, rings) for k in range(1, rings)])
+        gate_ref[...] = dot(weight(1, 1), full_in[...].reshape(width, tokens))
+        take(1, [lax.rem(mc + k, rings) for k in range(1, rings)])
+        gated_ref[...] = dot(weight(2, 1), full_grad[...].reshape(width, tokens))
+
+    x_in = full_in[...].reshape(width, tokens)
+    x_grad = full_grad[...].reshape(width, tokens)
+    gate = gate_ref[...]
+    d_gated = gated_ref[...]
+    took(got_mix, groups - 1, seq_recv.at[3])
+    mixed = by_token(got_mix[...])
+    d_gate = (d_gated * mixed).astype(BF16)
+    reduce_weights(gate, d_gated, d_gate, mixed, x_in, x_grad)
+    from_gate = lax.dot_general(weight(1, 1), d_gate, over_first, preferred_element_type=F32)
+
+    took(got_dv, groups - 1, seq_recv.at[4])
+    d_value = by_token(got_dv[...]).astype(BF16)
+    reduce_value(d_value, x_in)
+    d_in = lax.dot_general(weight(0, 1), d_value, over_first, preferred_element_type=F32) + from_gate
+    out_din[...] = d_in.reshape(rings, ch_rows, tokens).astype(BF16)
+    for k in range(1, rings):
+        block = lax.rem(mc + k, rings)
+        send(out_din.at[block], got_din.at[mc], (din_send.at[0], din_recv.at[0]), me, block).start()
+    got_din[mc] = out_din[mc]
 
     took(got_w, groups - 1, seq_recv.at[6])
     out_ws[...] = total(got_w)
@@ -414,12 +389,12 @@
     got_ws[me] = out_ws[...]
     got_v[me] = out_v[...]
 
-    when_count(seq_recv.at[5], got_df, groups - 1, groups)
+    took(got_df, groups - 1, seq_recv.at[5])
     dfil_ref[...] = by_token(got_df[...]).astype(BF16)
 
     took(got_v, groups - 1, seq_recv.at[8])
     dw_ref[0] = total(got_v)
-    when_count(din_recv.at[0], got_din, 1, 2)
+    took(got_din, rings - 1, din_recv.at[0])
     din_ref[...] = total(got_din)
     took(got_ws, groups - 1, seq_recv.at[7])
     size = parts * chans
@@ -441,22 +416,17 @@
 
     @pl.when(works)
     def _():
-        took(out_filt, groups - 1, seq_send.at[0])
-        for stage, src in ((1, out_val), (2, out_dif), (3, out_mix), (4, out_dv)):
-            took(src, groups - 1, seq_send.at[stage])
-        for stage, src in ((10, out_mix), (11, out_dv)):
-            took(src, (half - 1) * groups // half, seq_send.at[stage])
-        took(out_df, half * groups - 1, seq_send.at[5])
-        took(out_din, rings - 1, din_send.at[0])
+        for stage, src in ((1, out_val), (2, out_dif)):
+            took(src, half * groups - 1, seq_send.at[stage])
         for s in range(1, half):
             took(weights.at[s], splits - 1, share_send.at[s])
 
     @pl.when(rests)
     def _():
-        took(out_filt, groups, seq_send.at[0])
         share_up(slot).wait_send()
 
-    for stage, src in ((6, got_w), (7, got_ws), (8, got_v)):
+    took(out_din, rings - 1, din_send.at[0])
+    for stage, src in ((0, got_filt), (3, got_mix), (4, got_dv), (5, got_df), (6, got_w), (7, got_ws), (8, got_v)):
         took(src, groups - 1, seq_send.at[stage])
 
 
@@ -480,7 +450,6 @@
         vmem = pl.BlockSpec(memory_space=pltpu.VMEM)
         hbm = pl.BlockSpec(memory_space=pltpu.HBM)
         half = rings // 2
-        block = pltpu.VMEM((groups, half, tiles * chans, LANES), BF16)
         flat = pltpu.VMEM((half * groups, tiles * chans, LANES), BF16)
         plane = pltpu.VMEM((groups, tiles * chans, LANES), BF16)
         whole = pltpu.VMEM((rings, ch_rows, tokens), BF16)
@@ -501,9 +470,10 @@
             out_specs=(vmem,) * 3,
             scratch_shapes=[
                 whole, whole, pltpu.VMEM((ch_rows, tokens), F32), pltpu.VMEM((half, splits, 3, ch_rows // splits, width), BF16),
-                plane, flat] + [block] * 8 + [flat, plane]
-            + [whole, pltpu.VMEM((2, ch_rows, tokens), BF16)]
+                plane, plane, flat, plane, flat, plane] + [plane] * 6
+            + [whole, whole]
             + [share, share, pltpu.VMEM((2 * parts * chans, LANES), BF16), share, rows_of, pltpu.VMEM((groups, ch_rows, width), BF16)]
+            + [pltpu.VMEM((ch_rows, tokens), F32)] * 2
             + [pltpu.VMEM(table.shape, table.dtype) for table in tables] + [
                 pltpu.SemaphoreType.DMA((12,)),
                 pltpu.SemaphoreType.DMA((12,)),

time: 31.7 us -> 30.7 us (0.968)
  Pallas kernels: 30.9 us -> 29.9 us
    pallas_call x1, Pallas kernels: 30.2 us -> 29.1 us  [on_device(): pl.pallas_call(functools.partial(body, groups, rings), out_shape=(pltpu.V...]
where the time goes in v4:
time: 30.7 us; the launch traced here: 30.5 us
  Pallas kernels  29.9 us (97%)
  between operations  0.64 us (2%)
    pallas_call x1, Pallas kernels, on_device(): pl.pallas_call(functools.partial(body, groups, rings), out_shape=(pltpu.V...  29.1 us
    pallas_call x1, Pallas kernels, on_device(): pl.pallas_call(functools.partial(finish, scale), out_shape=(jax.ShapeDtyp...  0.76 us

profile of v4, /device:TPU:0, one launch (start us, length us, event | category | flops | bytes accessed | tf_op | source)
XLA Modules:
  0.0 30.5 jit_solution(4023105074956196925)
XLA Ops:
  0.6 29.1 %shard_map.146 = (bf16[64,512]{1,0:T(8,128)(2,1)S(1)}, bf16[3,64,256]{2,1,0:T(8,128)(2,1)S(1)}, bf16[64,512]{1,0:T(8,128)(2,1)S(1)}) custom-call(bf16[64,512]{1,0:T(8,128)(2,1)} %in_hbm.1, bf16[4,16,256]{2,1,0:T(8,128)(2,1)} %bitcast.9, bf16[4,16,256]{2,1,0:T(8,128)(2,1)} %bitcast.10, bf16[4,16,256]{2,1,0:T(8,128)(2,1)} %bitcast.11, f32[64,512]{1,0:T(8,128)} %filt_hbm.1, ...), custom_call_target="tpu_custom_call" | custom-call | tf_op jit(solution)/shard_map/pallas_call | solution.py:462
  29.7 0.8 %shard_map.147 = (bf16[64,512]{1,0:T(8,128)(2,1)}, f32[64,256]{1,0:T(8,128)}, f32[64,256]{1,0:T(8,128)}, f32[64,256]{1,0:T(8,128)}, f32[64,512]{1,0:T(8,128)}) custom-call(bf16[64,512]{1,0:T(8,128)(2,1)S(1)} %get-tuple-element.13.din_ref, bf16[3,64,256]{2,1,0:T(8,128)(2,1)S(1)} %get-tuple-element.14.dw_ref, bf16[64,512]{1,0:T(8,128)(2,1)S(1)} %get-tuple-element.15.dfil_ref), custom_call_target="tpu_custom_call" | custom-call | tf_op jit(solution)/shard_map/pallas_call | solution.py:494

commit v5 on v4

--- a/solution.py
+++ b/solution.py
@@ -142,11 +142,16 @@
 
     def scatter(stage, src, dst, ch, skip, base=0):
         each(groups - skip, lambda k: send(
-            src.at[base + seq_peer(k + skip)], dst, stage_sems(stage), seq_peer(k + skip), ch).start())
+            src.at[base + (me ^ (groups - 1 - k))], dst, stage_sems(stage), me ^ (groups - 1 - k), ch).start())
 
     def spread(stage, src, dst):
         each(groups - 1, lambda k: send(
-            src, dst.at[me], stage_sems(stage), seq_peer(k + 1), mc).start())
+            src, dst.at[me], stage_sems(stage), me ^ (groups - 1 - k), mc).start())
+
+    def to_plane(stage, src, dst, s):
+        scatter(stage, src, dst.at[me], mc - toward * s, 1 if s == 0 else 0, s * groups)
+        if s == 0:
+            dst[me] = src[me]
 
     def to_planes(stage, src, dst):
         for s in range(half):
@@ -290,6 +295,9 @@
 
     def weight(kind, count):
         return jnp.concatenate([weights[s, q, kind] for s in range(count) for q in range(splits)], axis=0)
+
+    def weight_of(kind, s):
+        return jnp.concatenate([weights[s, q, kind] for q in range(splits)], axis=0)
 
     def reduce_weights(gate, d_gated, d_gate, mixed, x_in, x_grad):
         gated_out = (gate[:ch_rows] * mixed[:ch_rows]).astype(BF16)
@@ -325,16 +333,20 @@
             across = weights.at[s, pl.ds(0, splits - 1)]
             pltpu.make_async_copy(across, across, share_recv.at[s, 1]).wait()
         x_in = full_in[...].reshape(width, tokens)
-        put_flat(out_val, [by_owner(x) for x in slots(dot(weight(0, half), x_in))])
-        to_planes(1, out_val, got_val)
-        gate = dot(weight(1, half), x_in)
-        gate_ref[...] = gate[:ch_rows]
+        order = list(reversed(range(half)))
+        for s in order:
+            out_val[s * groups:(s + 1) * groups] = by_owner(dot(weight_of(0, s), x_in))
+            to_plane(1, out_val, got_val, s)
+        gates = {s: dot(weight_of(1, s), x_in) for s in order}
+        gate_ref[...] = gates[0]
         take(1, outer_blocks + far_blocks)
         x_grad = full_grad[...].reshape(width, tokens)
-        d_gated = dot(weight(2, half), x_grad)
-        put_flat(out_dif, [by_owner(x) for x in slots(d_gated * gate)])
-        to_planes(2, out_dif, got_dif)
-        gated_ref[...] = d_gated[:ch_rows]
+        for s in order:
+            d_gated = dot(weight_of(2, s), x_grad)
+            out_dif[s * groups:(s + 1) * groups] = by_owner(d_gated * gates[s])
+            to_plane(2, out_dif, got_dif, s)
+            if s == 0:
+                gated_ref[...] = d_gated
         for array in range(2):
             for block in far_blocks:
                 pass_on(array, block)

time: 30.7 us -> 30.1 us (0.980)
  Pallas kernels: 29.9 us -> 29.3 us
    pallas_call x1, Pallas kernels: 29.1 us -> 28.5 us  [on_device(): pl.pallas_call(functools.partial(body, groups, rings), out_shape=(pltpu.V...]
where the time goes in v5:
time: 30.1 us; the launch traced here: 29.9 us
  Pallas kernels  29.3 us (97%)
  between operations  0.64 us (2%)
    pallas_call x1, Pallas kernels, on_device(): pl.pallas_call(functools.partial(body, groups, rings), out_shape=(pltpu.V...  28.5 us
    pallas_call x1, Pallas kernels, on_device(): pl.pallas_call(functools.partial(finish, scale), out_shape=(jax.ShapeDtyp...  0.76 us

profile of v5, /device:TPU:0, one launch (start us, length us, event | category | flops | bytes accessed | tf_op | source)
XLA Modules:
  0.0 29.9 jit_solution(11326157010127529347)
XLA Ops:
  0.6 28.5 %shard_map.146 = (bf16[64,512]{1,0:T(8,128)(2,1)S(1)}, bf16[3,64,256]{2,1,0:T(8,128)(2,1)S(1)}, bf16[64,512]{1,0:T(8,128)(2,1)S(1)}) custom-call(bf16[64,512]{1,0:T(8,128)(2,1)} %in_hbm.1, bf16[4,16,256]{2,1,0:T(8,128)(2,1)} %bitcast.9, bf16[4,16,256]{2,1,0:T(8,128)(2,1)} %bitcast.10, bf16[4,16,256]{2,1,0:T(8,128)(2,1)} %bitcast.11, f32[64,512]{1,0:T(8,128)} %filt_hbm.1, ...), custom_call_target="tpu_custom_call" | custom-call | tf_op jit(solution)/shard_map/pallas_call | solution.py:474
  29.2 0.8 %shard_map.147 = (bf16[64,512]{1,0:T(8,128)(2,1)}, f32[64,256]{1,0:T(8,128)}, f32[64,256]{1,0:T(8,128)}, f32[64,256]{1,0:T(8,128)}, f32[64,512]{1,0:T(8,128)}) custom-call(bf16[64,512]{1,0:T(8,128)(2,1)S(1)} %get-tuple-element.13.din_ref, bf16[3,64,256]{2,1,0:T(8,128)(2,1)S(1)} %get-tuple-element.14.dw_ref, bf16[64,512]{1,0:T(8,128)(2,1)S(1)} %get-tuple-element.15.dfil_ref), custom_call_target="tpu_custom_call" | custom-call | tf_op jit(solution)/shard_map/pallas_call | solution.py:506

commit v6 on v5

--- a/solution.py
+++ b/solution.py
@@ -56,7 +56,7 @@
     din_ref, dw_ref, dfil_ref,
     full_in, full_grad, filt_ref, weights, out_filt, got_filt, out_val, got_val, out_dif, got_dif,
     out_mix, got_mix, out_dv, got_dv, out_df, got_df,
-    out_din, got_din, out_w, got_w, out_ws, got_ws, out_v, got_v, gate_ref, gated_ref,
+    out_din, got_din, out_w, got_w, out_ws, got_ws, out_v, got_v, pair_ref, sum_ref, gate_ref, gated_ref,
     ahead_ref, back_ref, across_ref, return_ref, twist_ref,
     seq_send, seq_recv, din_send, din_recv, line_send, line_recv, share_send, share_recv,
     table_sem, fetch_sem, round_sem,
@@ -78,6 +78,7 @@
     works = slot == 0
     rests = slot > 0
     between = (mc > 0) & (mc < rings - 1)
+    core = lax.rem(me, 2)
     barrier = pltpu.get_barrier_semaphore()
     hops = near(groups)
 
@@ -306,10 +307,20 @@
         out_w[...] = jnp.concatenate([by_share(gate_term), by_share(out_term)], axis=1).astype(BF16)
         exchange(6, out_w, got_w)
 
+    def pair_copy():
+        return send(
+            out_v.at[1 - core], pair_ref, stage_sems(9), me ^ 1, mc)
+
     def reduce_value(d_value, x_in):
         value_term = lax.dot_general(d_value[:ch_rows], x_in, over_last, preferred_element_type=F32)
-        out_v[...] = value_term.astype(BF16)
-        spread(8, out_v, got_v)
+        out_v[...] = value_term.reshape(2, ch_rows // 2, width).astype(BF16)
+        pair_copy().start()
+
+    def spread_value():
+        pair_copy().wait_recv()
+        sum_ref[...] = (out_v[core].astype(F32) + pair_ref[...].astype(F32)).astype(BF16)
+        spread(8, sum_ref, got_v)
+        got_v[me] = sum_ref[...]
 
     over_first = (((0,), (0,)), ((), ()))
     over_last = (((1,), (1,)), ((), ()))
@@ -393,19 +404,23 @@
     for k in range(1, rings):
         block = lax.rem(mc + k, rings)
         send(out_din.at[block], got_din.at[mc], (din_send.at[0], din_recv.at[0]), me, block).start()
+    spread_value()
     got_din[mc] = out_din[mc]
 
     took(got_w, groups - 1, seq_recv.at[6])
     out_ws[...] = total(got_w)
     spread(7, out_ws, got_ws)
     got_ws[me] = out_ws[...]
-    got_v[me] = out_v[...]
 
     took(got_df, groups - 1, seq_recv.at[5])
     dfil_ref[...] = by_token(got_df[...]).astype(BF16)
 
     took(got_v, groups - 1, seq_recv.at[8])
-    dw_ref[0] = total(got_v)
+    for part in range(2):
+        half_sum = got_v[part].astype(F32)
+        for p in range(part + 2, groups, 2):
+            half_sum = half_sum + got_v[p].astype(F32)
+        dw_ref[0, part * (ch_rows // 2):(part + 1) * (ch_rows // 2)] = half_sum.astype(BF16)
     took(got_din, rings - 1, din_recv.at[0])
     din_ref[...] = total(got_din)
     took(got_ws, groups - 1, seq_recv.at[7])
@@ -437,6 +452,7 @@
     def _():
         share_up(slot).wait_send()
 
+    pair_copy().wait_send()
     took(out_din, rings - 1, din_send.at[0])
     for stage, src in ((0, got_filt), (3, got_mix), (4, got_dv), (5, got_df), (6, got_w), (7, got_ws), (8, got_v)):
         took(src, groups - 1, seq_send.at[stage])
@@ -468,7 +484,8 @@
         splits = min(groups, ch_rows // 16)
         split = lambda w: w.reshape(splits, ch_rows // splits, width)
         share = pltpu.VMEM((groups, 2 * parts * chans, LANES), BF16)
-        rows_of = pltpu.VMEM((ch_rows, width), BF16)
+        rows_of = pltpu.VMEM((ch_rows // 2, width), BF16)
+        pair_of = pltpu.VMEM((2, ch_rows // 2, width), BF16)
         tokens_out = jax.ShapeDtypeStruct((ch_rows, tokens), F32)
         weight_out = jax.ShapeDtypeStruct((ch_rows, width), F32)
         d_inputs, d_weights, d_filter = pl.pallas_call(
@@ -484,7 +501,7 @@
                 whole, whole, pltpu.VMEM((ch_rows, tokens), F32), pltpu.VMEM((half, splits, 3, ch_rows // splits, width), BF16),
                 plane, plane, flat, plane, flat, plane] + [plane] * 6
             + [whole, whole]
-            + [share, share, pltpu.VMEM((2 * parts * chans, LANES), BF16), share, rows_of, pltpu.VMEM((groups, ch_rows, width), BF16)]
+            + [share, share, pltpu.VMEM((2 * parts * chans, LANES), BF16), share, pair_of, pltpu.VMEM((groups, ch_rows // 2, width), BF16), rows_of, rows_of]
             + [pltpu.VMEM((ch_rows, tokens), F32)] * 2
             + [pltpu.VMEM(table.shape, table.dtype) for table in tables] + [
                 pltpu.SemaphoreType.DMA((12,)),

time: 30.1 us -> 29.9 us (level)
  no operation moved by 1% of the time
where the time goes in v6:
time: 29.9 us; the launch traced here: 29.7 us
  Pallas kernels  29.1 us (97%)
  between operations  0.64 us (2%)
    pallas_call x1, Pallas kernels, on_device(): pl.pallas_call(functools.partial(body, groups, rings), out_shape=(pltpu.V...  28.3 us
    pallas_call x1, Pallas kernels, on_device(): pl.pallas_call(functools.partial(finish, scale), out_shape=(jax.ShapeDtyp...  0.76 us

profile of v6, /device:TPU:0, one launch (start us, length us, event | category | flops | bytes accessed | tf_op | source)
XLA Modules:
  0.0 29.7 jit_solution(16964388697099472605)
XLA Ops:
  0.6 28.3 %shard_map.146 = (bf16[64,512]{1,0:T(8,128)(2,1)S(1)}, bf16[3,64,256]{2,1,0:T(8,128)(2,1)S(1)}, bf16[64,512]{1,0:T(8,128)(2,1)S(1)}) custom-call(bf16[64,512]{1,0:T(8,128)(2,1)} %in_hbm.1, bf16[4,16,256]{2,1,0:T(8,128)(2,1)} %bitcast.9, bf16[4,16,256]{2,1,0:T(8,128)(2,1)} %bitcast.10, bf16[4,16,256]{2,1,0:T(8,128)(2,1)} %bitcast.11, f32[64,512]{1,0:T(8,128)} %filt_hbm.1, ...), custom_call_target="tpu_custom_call" | custom-call | tf_op jit(solution)/shard_map/pallas_call | solution.py:491
  29.0 0.8 %shard_map.147 = (bf16[64,512]{1,0:T(8,128)(2,1)}, f32[64,256]{1,0:T(8,128)}, f32[64,256]{1,0:T(8,128)}, f32[64,256]{1,0:T(8,128)}, f32[64,512]{1,0:T(8,128)}) custom-call(bf16[64,512]{1,0:T(8,128)(2,1)S(1)} %get-tuple-element.13.din_ref, bf16[3,64,256]{2,1,0:T(8,128)(2,1)S(1)} %get-tuple-element.14.dw_ref, bf16[64,512]{1,0:T(8,128)(2,1)S(1)} %get-tuple-element.15.dfil_ref), custom_call_target="tpu_custom_call" | custom-call | tf_op jit(solution)/shard_map/pallas_call | solution.py:523
